TPU v7x, 512 devices: a whole 4x8x8 slice. The times are simulated.
512 devices in a mesh: grp: 8 (over z), row: 64 (over y, x, core).
Axes of the slice: x: 4, y: 8, z: 8, core: 2. Of those that a mesh axis runs over, the one named last changes fastest.
Arguments:
- tiles: bfloat16 [3072, 512, 512], P(('grp', 'row')), may hold values from -0.15625 to 0.15625
- tile_row: int32 [3072], P(('grp', 'row')), may hold values from 0 to 1023, as said below
- tile_col: int32 [3072], P(('grp', 'row')), may hold values from 0 to 1023, as said below
- tile_count: int32 [512], P(('grp', 'row')), may hold values from 3 to 6, as said below
- q_block: bfloat16 [524288, 256], P(('grp', 'row')), may hold values from -80 to 80
Outputs:
- q_next: float32 [524288, 256], P(('grp', 'row'))
Inputs may be any that keep to these rules, and one draw needn't show every extreme that they name: `tile_row`: each slot names one of its device's tile rows: d * 2 to d * 2 + 1 for device d. `tile_col`: each slot's tile column is (tile_row + o) mod 1024 with o from minus 2 to 2; no two slots of one device name the same pair of tile row and tile column. `tile_count`: some device has all 6 slots live.
All inputs are finite; a program needn't handle non-finite values.
Results may differ from a plain program's by a relative error of at most 0.0029.
Values may be sent and summed in bfloat16 or wider, within the bound.
No kernel may reach another device: no remote copies, remote signals or barrier semaphores. Data moves between devices by JAX's collectives and lax.ppermute only.
A program may use at most 64 MiB of HBM per device.

v0:
```python
import jax
import jax.numpy as jnp
from jax import lax
from jax.sharding import Mesh
from jax.sharding import PartitionSpec as P

H = 2
ROW = ("row_0", "row_1", "row_2")
GRP_ROW = ("grp", "row_0", "row_1", "row_2")


def with_halo(x, sides, width):
    edges = {}
    for axis, dim in sides:
        peers, length = (lax.axis_size(axis), x.shape[dim])
        up = [(i, (i + 1) % peers) for i in range(peers)]
        last = lax.slice_in_dim(x, length - width, length, axis=dim)
        initial = lax.slice_in_dim(x, 0, width, axis=dim)
        edges[dim] = (
            lax.ppermute(last, axis, up),
            lax.ppermute(initial, axis, [(b, a) for a, b in up]),
        )
    done = []
    for _, dim in sides:
        low, high = edges[dim]
        around = [(width, width) if d in done else (0, 0) for d in range(x.ndim)]
        x = jnp.concatenate([jnp.pad(low, around), x, jnp.pad(high, around)], axis=dim)
        done.append(dim)
    return x


def split_up(x, dim, peers):
    lengths = x.shape
    tiles = x.reshape(*lengths[:dim], peers, lengths[dim] // peers, *lengths[dim + 1 :])
    return jnp.moveaxis(tiles, dim, 0)


def summed_on_arrival(x, axis, dim):
    tiles = split_up(x, dim, lax.axis_size(axis))
    arrived = lax.all_to_all(tiles, axis, split_axis=0, concat_axis=0, tiled=True)
    return arrived.astype(jnp.float32).sum(axis=0)


def sum_in_two_steps(x, axes, dim):
    far, near = axes
    own = summed_on_arrival(split_up(x, dim, lax.axis_size(far)), near, dim + 1)
    return jnp.sum(
        lax.all_to_all(own.astype(jnp.bfloat16), far, 0, 0, tiled=True).astype(jnp.float32), axis=0
    )


def padded_to(lines, peers):
    spare = -len(lines) % peers
    return jnp.pad(lines, [(0, spare)] + [(0, 0)] * (lines.ndim - 1))


def from_everyone(x, axis):
    copies = jnp.broadcast_to(x, (lax.axis_size(axis), *x.shape))
    return lax.all_to_all(copies, axis, split_axis=0, concat_axis=0, tiled=True)


def in_order(tiles, dim):
    tiles = jnp.moveaxis(tiles, 0, dim)
    lengths = tiles.shape
    return tiles.reshape(*lengths[:dim], lengths[dim] * lengths[dim + 1], *lengths[dim + 2 :])


def gathered_by_axis(x, axes, dim):
    far, near = axes
    tiles = from_everyone(from_everyone(x, far), near)
    return in_order(tiles.swapaxes(0, 1).reshape(-1, *x.shape), dim)


def nested_sum(x, axes):
    lines = x.reshape(-1)
    own = sum_in_two_steps(
        padded_to(lines, lax.axis_size(axes[0]) * lax.axis_size(axes[1])), axes, 0
    )
    whole = gathered_by_axis(own.astype(jnp.bfloat16), axes, 0)
    return whole[: len(lines)].reshape(x.shape).astype(jnp.float32)


def on_device(tiles, tile_row, tile_col, tile_count, q_block):
    slot_count, tile_size, unused_size = tiles.shape
    basis_width = q_block.shape[1]
    own_tiles = q_block.shape[0] // tile_size
    window = own_tiles + 2 * H
    tile_total = own_tiles * lax.axis_size("grp") * lax.axis_size(ROW)
    local_row = tile_row % own_tiles
    local_col = (tile_col - tile_row + H) % tile_total + local_row
    padded = with_halo(q_block, ((GRP_ROW, 0),), H * tile_size)
    stack = padded.reshape(window, tile_size, basis_width)
    live_slot = jnp.arange(slot_count, dtype=jnp.int32) < tile_count[0]
    blocks = stack[local_col]
    blocks = jnp.where(live_slot[:, None, None], blocks, jnp.zeros_like(blocks))
    products = jnp.einsum("sab,sbk->sak", tiles, blocks, preferred_element_type=jnp.float32)
    row_ids = jnp.arange(own_tiles, dtype=jnp.int32)
    row_place = ((local_row[None, :] == row_ids[:, None]) & live_slot[None, :]).astype(jnp.float32)
    aq_tiles = jnp.einsum(
        "rs,sak->rak", row_place, products, precision=lax.Precision.HIGHEST
    ).astype(jnp.bfloat16)
    row_part = aq_tiles[local_row]
    images = jnp.einsum("sab,sak->sbk", tiles, row_part, preferred_element_type=jnp.float32)
    column_ids = jnp.arange(window, dtype=jnp.int32)
    col_place = ((local_col[None, :] == column_ids[:, None]) & live_slot[None, :]).astype(
        jnp.float32
    )
    sums = jnp.einsum("cs,sbk->cbk", col_place, images, precision=lax.Precision.HIGHEST)
    own_part = sums[H : H + own_tiles]
    lower = sums[:H].astype(jnp.bfloat16).reshape(H * tile_size, basis_width)
    upper = sums[H + own_tiles :].astype(jnp.bfloat16).reshape(H * tile_size, basis_width)
    edges = with_halo(jnp.concatenate([lower, upper], axis=0), ((GRP_ROW, 0),), H * tile_size)
    from_below = edges[: H * tile_size]
    from_above = edges[edges.shape[0] - H * tile_size :]
    below_tiles = from_below.astype(jnp.float32).reshape(H, tile_size, basis_width)
    above_tiles = from_above.astype(jnp.float32).reshape(H, tile_size, basis_width)
    own_part = own_part + below_tiles
    own_part = own_part + above_tiles
    local_y = own_part.reshape(own_tiles * tile_size, basis_width)
    rows_total = tile_total * tile_size
    local_gram = jnp.dot(
        local_y.T, local_y, precision=lax.Precision.HIGHEST, preferred_element_type=jnp.float32
    )
    gram_matrix = (
        nested_sum(local_gram.astype(jnp.bfloat16), (("grp", "row_0"), ("row_1", "row_2")))
        / rows_total
    )
    factor_low = jnp.linalg.cholesky(gram_matrix)
    return lax.linalg.triangular_solve(
        factor_low, local_y, left_side=False, lower=True, transpose_a=True
    )


def solution(mesh):
    torus = Mesh(
        mesh.devices.reshape(mesh.shape["grp"], 8, 4, 2), ("grp", "row_0", "row_1", "row_2")
    )
    return jax.shard_map(
        on_device,
        mesh=torus,
        in_specs=(P(GRP_ROW, None, None), P(GRP_ROW), P(GRP_ROW), P(GRP_ROW), P(GRP_ROW, None)),
        out_specs=P(GRP_ROW, None),
        check_vma=False,
    )
```

profile of v0, /device:TPU:1, one launch (start us, length us, event | category | flops | bytes accessed | tf_op | source)
XLA Modules:
  0.0 215.5 jit_solution(11528828650594353785)
XLA Ops:
  0.0 4.8 %collective-permute-start = (bf16[1024,256]{1,0:T(8,128)(2,1)}, bf16[1024,256]{1,0:T(8,128)(2,1)S(1)}, u32[]{:S(2)}, u32[]{:S(2)}) collective-permute-start(bf16[1024,256]{1,0:T(8,128)(2,1)} %param.9), channel_id=1, source_target_pairs={{0,1},{1,2},{2,3},{3,4},{4,5},{5,6},{6,7},{7,8},{8,9},{9,10},{10,1... | collective-permute-start | bytes 1572872 | tf_op jit(solution)/shard_map/ppermute | solution.py:20
  4.8 6.2 %collective-permute-start.1 = (bf16[1024,256]{1,0:T(8,128)(2,1)}, bf16[1024,256]{1,0:T(8,128)(2,1)S(1)}, u32[]{:S(2)}, u32[]{:S(2)}) collective-permute-start(bf16[1024,256]{1,0:T(8,128)(2,1)} %param.9), channel_id=1, source_target_pairs={{1,0},{2,1},{3,2},{4,3},{5,4},{6,5},{7,6},{8,7},{9,8},{10,9},{11,1... | collective-permute-start | bytes 1572872 | tf_op jit(solution)/shard_map/ppermute | solution.py:21
  13.0 2.5 %collective-permute-done.1 = bf16[1024,256]{1,0:T(8,128)(2,1)S(1)} collective-permute-done((bf16[1024,256]{1,0:T(8,128)(2,1)}, bf16[1024,256]{1,0:T(8,128)(2,1)S(1)}, u32[]{:S(2)}, u32[]{:S(2)}) %collective-permute-start.1) | collective-permute-done | bytes 524320 | tf_op jit(solution)/shard_map/ppermute | solution.py:21
  15.5 2.3 %pad_maximum_fusion = bf16[3072,256]{1,0:T(8,128)(2,1)} fusion(bf16[1024,256]{1,0:T(8,128)(2,1)S(1)} %collective-permute-done.1, bf16[1024,256]{1,0:T(8,128)(2,1)} %param.9, bf16[1024,256]{1,0:T(8,128)(2,1)S(1)} %collective-permute-done), kind=kLoop, calls=%fused_computation.6 | loop fusion | flops 4718592 | bytes 3145728 | tf_op jit(solution)/shard_map/concatenate | solution.py:27
  17.8 3.3 %gather_fusion = bf16[6,512,256]{2,1,0:T(8,128)(2,1)} fusion(bf16[6,512,256]{2,1,0:T(8,128)(2,1)} %bitcast.74, s32[1024]{0:T(1024)S(1)} %pad_clamp_fusion.1), kind=kCustom, calls=%fused_computation | custom fusion | bytes 3145752 | tf_op jit(solution)/shard_map/gather | solution.py:94
  21.1 4.3 %convolution_bitcast_fusion.1 = f32[6,512,256]{1,2,0:T(8,128)} fusion(bf16[6,512,512]{2,1,0:T(8,128)(2,1)S(1)} %copy-done, bf16[6,512,256]{2,1,0:T(8,128)(2,1)} %gather_fusion, pred[6]{0:T(512)(128)(4,1)S(1)} %iota_compare_fusion.4), kind=kOutput, calls=%fused_computation.5 | convolution fusion | flops 806092800 | bytes 7864326 | tf_op jit(solution)/shard_map/sab,sbk->sak/dot_general | solution.py:96
  25.3 5.1 %copy.51 = f32[6,512,256]{2,0,1:T(8,128)} copy(f32[6,512,256]{1,2,0:T(8,128)} %convolution_bitcast_fusion.1) | data formatting | bytes 6291456 | tf_op jit(solution)/shard_map/sab,sbk->sak/dot_general | solution.py:96
  30.4 4.3 %convolution_convert_fusion = bf16[2,512,256]{2,0,1:T(2,128)(2,1)S(1)} fusion(f32[6,512,256]{2,0,1:T(8,128)} %copy.51, pred[6]{0:T(512)(128)(4,1)S(1)} %iota_compare_fusion.4, s32[6]{0:T(128)S(1)} %get-tuple-element.22), kind=kOutput, calls=%fused_computation.9 | convolution fusion | flops 19136536 | bytes 3670046 | tf_op jit(solution)/shard_map/rs,sak->rak/dot_general | solution.py:99
  35.6 2.9 %gather_fusion.1 = bf16[6,512,256]{2,1,0:T(8,128)(2,1)} fusion(bf16[2,512,256]{2,1,0:T(8,128)(2,1)} %copy.52, s32[1024]{0:T(1024)S(1)} %pad_clamp_fusion), kind=kCustom, calls=%fused_computation.1 | custom fusion | bytes 3145752 | tf_op jit(solution)/shard_map/gather | solution.py:102
  38.5 4.1 %convolution_bitcast_fusion = f32[6,512,256]{1,2,0:T(8,128)} fusion(bf16[6,512,256]{2,1,0:T(8,128)(2,1)} %gather_fusion.1, bf16[6,512,512]{2,1,0:T(8,128)(2,1)S(1)} %copy-done), kind=kOutput, calls=%fused_computation.4 | convolution fusion | flops 805306368 | bytes 7864320 | tf_op jit(solution)/shard_map/sab,sak->sbk/dot_general | solution.py:103
  42.6 5.1 %copy.54 = f32[6,512,256]{2,0,1:T(8,128)} copy(f32[6,512,256]{1,2,0:T(8,128)} %convolution_bitcast_fusion) | data formatting | bytes 6291456 | tf_op jit(solution)/shard_map/sab,sak->sbk/dot_general | solution.py:103
  47.7 4.3 %fusion.33 = (bf16[6,512,256]{2,0,1:T(8,128)(2,1)S(1)}, f32[6,512,256]{2,0,1:T(8,128)S(1)}) fusion(f32[6,512,256]{2,0,1:T(8,128)} %copy.54, s32[6]{0:T(128)S(1)} %get-tuple-element.24, pred[6]{0:T(512)(128)(4,1)S(1)} %iota_compare_fusion.4), kind=kOutput, calls=%fused_computation.74 | convolution fusion | flops 57409608 | bytes 7864350 | tf_op jit(solution)/shard_map/cs,sbk->cbk/dot_general | solution.py:108
  54.8 12.6 %collective-permute-start.3 = (bf16[1024,256]{1,0:T(8,128)(2,1)S(1)}, bf16[1024,256]{1,0:T(8,128)(2,1)S(1)}, u32[]{:S(2)}, u32[]{:S(2)}) collective-permute-start(bf16[1024,256]{1,0:T(8,128)(2,1)S(1)} %bitcast.76), channel_id=1, source_target_pairs={{1,0},{2,1},{3,2},{4,3},{5,4},{6,5},{7,6},{8,7},{9,8},{10,9},{11,1... | collective-permute-start | bytes 1572872 | tf_op jit(solution)/shard_map/ppermute | solution.py:21
  72.0 20.2 %all_to_all.28 = bf16[8,64,128]{2,1,0:T(8,128)(2,1)S(1)} all-to-all(bf16[8,64,128]{2,1,0:T(8,128)(2,1)S(1)} %bitcast.77), channel_id=1, replica_groups=mesh['grp'=8,'row_0'=8,'row_1'=4,'row_2'=2] {'row_1','row_2'}, dimensions={0} | all-to-all | bytes 262144 | tf_op jit(solution)/shard_map/all_to_all | solution.py:40
  92.3 19.1 %all_to_all.29 = bf16[64,1,128]{2,1,0:T(2,128)(2,1)S(1)} all-to-all(bf16[64,1,128]{2,1,0:T(2,128)(2,1)S(1)} %copy.60), channel_id=1, replica_groups=mesh['grp'=8,'row_0'=8,'row_1'=4,'row_2'=2] {'grp','row_0'}, dimensions={0} | all-to-all | bytes 32768 | tf_op jit(solution)/shard_map/all_to_all | solution.py:48
  111.5 14.7 %all_to_all.30 = bf16[64,1,128]{2,1,0:T(2,128)(2,1)S(1)} all-to-all(bf16[64,1,128]{2,1,0:T(2,128)(2,1)S(1)} %broadcast_in_dim.36), channel_id=1, replica_groups=mesh['grp'=8,'row_0'=8,'row_1'=4,'row_2'=2] {'grp','row_0'}, dimensions={0} | all-to-all | bytes 32768 | tf_op jit(solution)/shard_map/all_to_all | solution.py:59
  126.8 6.7 %all-to-all-start.3 = ((bf16[8,64,128]{2,1,0:T(8,128)(2,1)}), bf16[8,64,128]{2,1,0:T(8,128)(2,1)S(1)}, u32[]{:S(2)}, u32[]{:S(2)}) async-start(bf16[8,64,128]{2,1,0:T(8,128)(2,1)} %broadcast_in_dim.37), calls=%async_computation.3 | async-start | bytes 262144 | tf_op jit(solution)/shard_map/all_to_all | solution.py:59
  133.5 5.3 %all-to-all-done.3 = bf16[8,64,128]{2,1,0:T(8,128)(2,1)S(1)} async-done(((bf16[8,64,128]{2,1,0:T(8,128)(2,1)}), bf16[8,64,128]{2,1,0:T(8,128)(2,1)S(1)}, u32[]{:S(2)}, u32[]{:S(2)}) %all-to-all-start.3) | async-done | bytes 131104 | tf_op jit(solution)/shard_map/all_to_all | solution.py:59
  143.2 11.7 %cholesky.50 = f32[128,128]{1,0:T(8,128)S(1)} custom-call(f32[128,128]{1,0:T(8,128)S(1)} %cholesky.118), custom_call_target="Cholesky" | custom-call | tf_op jit(solution)/shard_map/jit(cholesky)/cholesky | solution.py:128
  154.9 9.8 %custom-call.14 = f32[1,128,128]{1,2,0:T(8,128)S(1)} custom-call(f32[1,128,128]{2,1,0:T(8,128)S(1)} %get-tuple-element.32), custom_call_target="InvertDiagBlocksLowerTriangular" | custom-call | tf_op jit(solution)/shard_map/jit(cholesky)/cholesky | solution.py:128
  166.9 11.7 %cholesky.105 = f32[128,128]{1,0:T(8,128)S(1)} custom-call(f32[128,128]{1,0:T(8,128)S(1)} %convolution_subtract_fusion), custom_call_target="Cholesky" | custom-call | tf_op jit(solution)/shard_map/jit(cholesky)/cholesky | solution.py:128
  181.8 5.2 %while.1 = (s32[]{:T(128)}, f32[256,256]{1,0:T(8,128)S(1)}, s32[2,2]{1,0:T(2,128)S(1)}, f32[2,128,128]{2,1,0:T(8,128)}, s32[]{:T(128)}) while((s32[]{:T(128)}, f32[256,256]{1,0:T(8,128)S(1)}, s32[2,2]{1,0:T(2,128)S(1)}, f32[2,128,128]{2,1,0:T(8,128)}, s32[]{:T(128)}) %tuple.27), condition=%wide.while_cond, body=%wide.while_body.sunk | while | flops 2 | bytes 132705 | solution.py:129
  187.1 20.5 %custom-call.15 = f32[2,128,128]{1,2,0:T(8,128)S(1)} custom-call(f32[2,128,128]{2,1,0:T(8,128)} %get-tuple-element.12), custom_call_target="InvertDiagBlocksLowerTriangular" | custom-call | tf_op jit(solution)/shard_map/triangular_solve | solution.py:129
  213.0 2.5 %copy.63 = f32[1024,256]{1,0:T(8,128)} copy(f32[1024,256]{0,1:T(8,128)} %pad_maximum_fusion.1) | data formatting | bytes 2097152 | tf_op jit(solution)/shard_map/triangular_solve | solution.py:129
  (58 shorter events, 29.4 us)
Async XLA Ops:
  0.0 21.1 %copy-start = (bf16[6,512,512]{2,1,0:T(8,128)(2,1)S(1)}, bf16[6,512,512]{2,1,0:T(8,128)(2,1)}, u32[]{:S(2)}) copy-start(bf16[6,512,512]{2,1,0:T(8,128)(2,1)} %param.5) | copy-start | bytes 9437188
  0.0 13.0 %collective-permute-start = (bf16[1024,256]{1,0:T(8,128)(2,1)}, bf16[1024,256]{1,0:T(8,128)(2,1)S(1)}, u32[]{:S(2)}, u32[]{:S(2)}) collective-permute-start(bf16[1024,256]{1,0:T(8,128)(2,1)} %param.9), channel_id=1, source_target_pairs={{0,1},{1,2},{2,3},{3,4},{4,5},{5,6},{6,7},{7,8},{8,9},{9,10},{10,1... | collective-permute-start | bytes 1572872 | tf_op jit(solution)/shard_map/ppermute | solution.py:20
  4.8 10.7 %collective-permute-start.1 = (bf16[1024,256]{1,0:T(8,128)(2,1)}, bf16[1024,256]{1,0:T(8,128)(2,1)S(1)}, u32[]{:S(2)}, u32[]{:S(2)}) collective-permute-start(bf16[1024,256]{1,0:T(8,128)(2,1)} %param.9), channel_id=1, source_target_pairs={{1,0},{2,1},{3,2},{4,3},{5,4},{6,5},{7,6},{8,7},{9,8},{10,9},{11,1... | collective-permute-start | bytes 1572872 | tf_op jit(solution)/shard_map/ppermute | solution.py:21
  52.8 15.2 %collective-permute-start.2 = (bf16[1024,256]{1,0:T(8,128)(2,1)S(1)}, bf16[1024,256]{1,0:T(8,128)(2,1)S(1)}, u32[]{:S(2)}, u32[]{:S(2)}) collective-permute-start(bf16[1024,256]{1,0:T(8,128)(2,1)S(1)} %bitcast.75), channel_id=1, source_target_pairs={{0,1},{1,2},{2,3},{3,4},{4,5},{5,6},{6,7},{7,8},{8,9},{9,10},{10,1... | collective-permute-start | bytes 1572872 | tf_op jit(solution)/shard_map/ppermute | solution.py:20
  54.8 14.1 %collective-permute-start.3 = (bf16[1024,256]{1,0:T(8,128)(2,1)S(1)}, bf16[1024,256]{1,0:T(8,128)(2,1)S(1)}, u32[]{:S(2)}, u32[]{:S(2)}) collective-permute-start(bf16[1024,256]{1,0:T(8,128)(2,1)S(1)} %bitcast.76), channel_id=1, source_target_pairs={{1,0},{2,1},{3,2},{4,3},{5,4},{6,5},{7,6},{8,7},{9,8},{10,9},{11,1... | collective-permute-start | bytes 1572872 | tf_op jit(solution)/shard_map/ppermute | solution.py:21
  69.1 1.0 copy-start.1
  126.8 12.0 %all-to-all-start.3 = ((bf16[8,64,128]{2,1,0:T(8,128)(2,1)}), bf16[8,64,128]{2,1,0:T(8,128)(2,1)S(1)}, u32[]{:S(2)}, u32[]{:S(2)}) async-start(bf16[8,64,128]{2,1,0:T(8,128)(2,1)} %broadcast_in_dim.37), calls=%async_computation.3 | async-start | bytes 262144 | tf_op jit(solution)/shard_map/all_to_all | solution.py:59
  142.5 0.7 copy-start.3
  178.7 2.1 copy-start.2
where the time goes:
time: 217 us; the launch traced here: 216 us
  other arithmetic  61.5 us (28%)
  blocking collectives  54 us (25%)
  starting transfers between devices  32.2 us (15%)
  local copies, waits for them, and re-layouts  31.6 us (15%)
  matrix products  25.3 us (12%)
  waiting for transfers between devices  8.7 us (4%)
  between operations  2.28 us (1%)
    another operation x6, other arithmetic, on_device(): factor_low = jnp.linalg.cholesky(gram_matrix)  34 us
    another operation x4, other arithmetic, on_device(): lax.linalg.triangular_solve(factor_low, local_y, left_side=False, lower=T...  22.5 us
    all_to_all x1, blocking collectives, summed_on_arrival(): lax.all_to_all(tiles, axis, split_axis=0, concat_axis=0, tiled=True)  20.2 us
    all_to_all x1, blocking collectives, sum_in_two_steps(): lax.all_to_all(own.astype(jnp.bfloat16), far, 0, 0, tiled=True)  19.1 us
    ppermute x2, starting transfers between devices, with_halo(): lax.ppermute(initial, axis, [(b, a) for a, b in up])  18.8 us
    all_to_all x1, blocking collectives, from_everyone(): return lax.all_to_all(copies, axis, split_axis=0, concat_axis=0, tiled=True)  14.7 us
    all_to_all x1, starting transfers between devices, from_everyone(): return lax.all_to_all(copies, axis, split_axis=0, concat_axis=0, tiled=True)  6.72 us
    ppermute x2, starting transfers between devices, with_halo(): lax.ppermute(last, axis, up)  6.67 us
  transfers between devices with their start and end apart: 5, of which 3 were waited for; matrix products, arithmetic and copies ran while one was open for 1% of the time, Pallas kernels for 0%

commit v1 on v0

v1 whole, which is shorter than its diff:
```python
import functools

import jax
import jax.numpy as jnp
from jax import lax
from jax.experimental import pallas as pl
from jax.experimental.pallas import tpu as pltpu
from jax.sharding import Mesh
from jax.sharding import PartitionSpec as P

H = 2
LEAF = 64
AXES = ("grp", "y", "x", "core")
F32 = jnp.float32
BF16 = jnp.bfloat16
HIGHEST = lax.Precision.HIGHEST


def dot(a, b, ca, cb, precision=None):
    return lax.dot_general(
        a, b, (((ca,), (cb,)), ((), ())), precision=precision, preferred_element_type=F32
    )


def band_kernel(
    nt, row_ref, col_ref, count_ref, tiles_ref, low_ref, q_ref, high_ref,
    own_ref, lower_ref, upper_ref, win, acc, terms, aq,
):
    slots, bs, _ = tiles_ref.shape
    own = q_ref.shape[0] // bs
    for c in range(H):
        win[c] = low_ref[pl.ds(c * bs, bs), :]
        win[H + own + c] = high_ref[pl.ds(c * bs, bs), :]
    for c in range(own):
        win[H + c] = q_ref[pl.ds(c * bs, bs), :]
    acc[...] = jnp.zeros_like(acc)
    terms[...] = jnp.zeros_like(terms)

    def place(s):
        row = row_ref[s]
        off = col_ref[s] - row + H
        off = jnp.where(off < 0, off + nt, off)
        off = jnp.where(off >= nt, off - nt, off)
        row = lax.rem(row, own)
        return row, row + off

    for s in range(slots):

        @pl.when(s < count_ref[0])
        def _():
            row, col = place(s)
            acc[row] += dot(tiles_ref[s], win[col], 1, 0)

    aq[...] = acc[...].astype(BF16)
    for s in range(slots):

        @pl.when(s < count_ref[0])
        def _():
            row, col = place(s)
            terms[col] += dot(tiles_ref[s], aq[row], 0, 0)

    for c in range(H):
        lower_ref[pl.ds(c * bs, bs), :] = terms[c].astype(BF16)
        upper_ref[pl.ds(c * bs, bs), :] = terms[H + own + c].astype(BF16)
    for c in range(own):
        own_ref[pl.ds(c * bs, bs), :] = terms[H + c]


def band(nt, tiles, tile_row, tile_col, tile_count, low, q, high):
    slots, bs, _ = tiles.shape
    rows, k = q.shape
    own = rows // bs
    smem = pl.BlockSpec(memory_space=pltpu.SMEM)
    vmem = pl.BlockSpec(memory_space=pltpu.VMEM)
    return pl.pallas_call(
        functools.partial(band_kernel, nt),
        out_shape=(
            jax.ShapeDtypeStruct((rows, k), F32),
            jax.ShapeDtypeStruct((H * bs, k), BF16),
            jax.ShapeDtypeStruct((H * bs, k), BF16),
        ),
        in_specs=[smem] * 3 + [vmem] * 4,
        out_specs=(vmem,) * 3,
        scratch_shapes=[
            pltpu.VMEM((own + 2 * H, bs, k), BF16),
            pltpu.VMEM((own, bs, k), F32),
            pltpu.VMEM((own + 2 * H, bs, k), F32),
            pltpu.VMEM((own, bs, k), BF16),
        ],
        compiler_params=pltpu.CompilerParams(vmem_limit_bytes=32 << 20),
        cost_estimate=pl.CostEstimate(
            flops=4 * slots * bs * bs * k, bytes_accessed=tiles.size * 2, transcendentals=0
        ),
        name="band",
    )(tile_row, tile_col, tile_count, tiles, low, q, high)


def gram_kernel(own_ref, below_ref, above_ref, y_ref, gram_ref):
    y = own_ref[...] + below_ref[...].astype(F32) + above_ref[...].astype(F32)
    y_ref[...] = y
    b = y.astype(BF16)
    half = b.shape[1] // 2
    full = dot(b, b, 0, 0)
    gram_ref[0:half, :] = full[:half, :half].astype(BF16)
    gram_ref[half : 2 * half, :] = full[:half, half:].astype(BF16)
    gram_ref[2 * half :, :] = full[half:, half:].astype(BF16)


def gram(own, below, above):
    rows, k = own.shape
    vmem = pl.BlockSpec(memory_space=pltpu.VMEM)
    return pl.pallas_call(
        gram_kernel,
        out_shape=(
            jax.ShapeDtypeStruct((rows, k), F32),
            jax.ShapeDtypeStruct((3 * k // 2, k // 2), BF16),
        ),
        in_specs=[vmem] * 3,
        out_specs=(vmem,) * 2,
        compiler_params=pltpu.CompilerParams(vmem_limit_bytes=32 << 20),
        cost_estimate=pl.CostEstimate(
            flops=2 * rows * k * k, bytes_accessed=8 * rows * k, transcendentals=0
        ),
        name="gram",
    )(own, below, above)


def spread(piece):
    return jnp.broadcast_to(piece, (8, 128))


def leaf_inverse(d):
    n = d.shape[0]
    pieces = n // 8
    eye = (
        lax.broadcasted_iota(jnp.int32, (n, n), 0) == lax.broadcasted_iota(jnp.int32, (n, n), 1)
    ).astype(F32)
    both = jnp.concatenate([eye, d], axis=1)
    a = [both[8 * r : 8 * r + 8, :] for r in range(pieces)]
    line = lax.broadcasted_iota(jnp.int32, (8, 128), 0)
    for t in range(pieces):
        cols = [
            [spread(a[r][:, n + 8 * t + i : n + 8 * t + i + 1]) for r in range(t, pieces)]
            for i in range(8)
        ]
        pivots = jnp.ones((8, 128), F32)
        for i in range(8):
            pivot = spread(cols[i][0][i : i + 1, :])
            pivots = jnp.where(line == i, pivot, pivots)
            root = lax.rsqrt(pivot)
            scale = root * root
            by = [c * scale for c in cols[i]]
            by[0] = jnp.where(line > i, by[0], 0.0)
            for j in range(i + 1, 8):
                row = spread(cols[j][0][i : i + 1, :])
                cols[j] = [c - b * row for c, b in zip(cols[j], by)]
            row = spread(a[t][i : i + 1, :])
            for r, b in enumerate(by):
                a[t + r] = a[t + r] - b * row
        a[t] = a[t] * lax.rsqrt(pivots)
    return jnp.concatenate([piece[:, :n] for piece in a], axis=0)


def factor_inverse(g):
    g11, g12, g22 = g
    x11 = whole_inverse(g11)
    b = dot(x11, g12, 1, 0, HIGHEST)
    s = g22 - dot(b, b, 0, 0, HIGHEST)
    x22 = whole_inverse(s)
    x21 = -dot(x22, dot(b, x11, 0, 0, HIGHEST), 1, 0, HIGHEST)
    return x11, x21, x22


def whole_inverse(d):
    n = d.shape[0]
    if n == LEAF:
        return leaf_inverse(d)
    h = n // 2
    x11, x21, x22 = factor_inverse((d[:h, :h], d[:h, h:], d[h:, h:]))
    upper = jnp.concatenate([x11, jnp.zeros_like(x11)], axis=1)
    return jnp.concatenate([upper, jnp.concatenate([x21, x22], axis=1)], axis=0)


def split(x):
    hi = x.astype(BF16)
    return hi, (x - hi.astype(F32)).astype(BF16)


def next_kernel(rows_total, gram_ref, y_ref, out_ref):
    half = gram_ref.shape[1]
    g = [gram_ref[pl.ds(i * half, half), :].astype(F32) / rows_total for i in range(3)]
    x11, x21, x22 = factor_inverse(g)
    upper = jnp.concatenate([x11, jnp.zeros_like(x11)], axis=1)
    x = jnp.concatenate([upper, jnp.concatenate([x21, x22], axis=1)], axis=0)
    x_hi, x_lo = split(x)
    y_hi, y_lo = split(y_ref[...])
    out_ref[...] = dot(y_hi, x_hi, 1, 1) + (dot(y_lo, x_hi, 1, 1) + dot(y_hi, x_lo, 1, 1))


def next_basis(rows_total, packed, y):
    rows, k = y.shape
    vmem = pl.BlockSpec(memory_space=pltpu.VMEM)
    return pl.pallas_call(
        functools.partial(next_kernel, rows_total),
        out_shape=jax.ShapeDtypeStruct((rows, k), F32),
        in_specs=[vmem] * 2,
        out_specs=vmem,
        compiler_params=pltpu.CompilerParams(vmem_limit_bytes=32 << 20),
        cost_estimate=pl.CostEstimate(
            flops=6 * rows * k * k, bytes_accessed=8 * rows * k, transcendentals=0
        ),
        name="next_basis",
    )(packed, y)


def summed(x):
    return x.astype(F32).sum(axis=0).astype(BF16)


def exchange(x, axes):
    return lax.all_to_all(x, axes, split_axis=0, concat_axis=0, tiled=True)


def from_everyone(x, axes):
    return exchange(jnp.broadcast_to(x, (lax.axis_size(axes), *x.shape)), axes)


def sum_everywhere(x):
    near = ("x", "core")
    parts = x.reshape(lax.axis_size(near), -1, x.shape[1])
    own = summed(exchange(parts, near))
    own = summed(from_everyone(own, "y"))
    own = summed(from_everyone(own, "grp"))
    return from_everyone(own, near).reshape(x.shape)


def on_device(tiles, tile_row, tile_col, tile_count, q_block):
    bs = tiles.shape[1]
    peers = lax.axis_size(AXES)
    rows = q_block.shape[0]
    up = [(i, (i + 1) % peers) for i in range(peers)]
    down = [(b, a) for a, b in up]
    low = lax.ppermute(q_block[rows - H * bs :], AXES, up)
    high = lax.ppermute(q_block[: H * bs], AXES, down)
    own, lower, upper = band(
        rows // bs * peers, tiles, tile_row, tile_col, tile_count, low, q_block, high
    )
    below = lax.ppermute(upper, AXES, up)
    above = lax.ppermute(lower, AXES, down)
    y, packed = gram(own, below, above)
    return next_basis(rows * peers, sum_everywhere(packed), y)


def solution(mesh):
    torus = Mesh(mesh.devices.reshape(mesh.shape["grp"], 8, 4, 2), AXES)
    return jax.shard_map(
        on_device,
        mesh=torus,
        in_specs=(P(AXES, None, None), P(AXES), P(AXES), P(AXES), P(AXES, None)),
        out_specs=P(AXES, None),
        check_vma=False,
    )
```

time: 217 us -> 107 us (0.49)
  other arithmetic: 61.5 us -> 0.06 us
  local copies, waits for them, and re-layouts: 31.6 us -> 4.29 us
  matrix products: 25.3 us -> 0 us
  Pallas kernels: 0 us -> 16.6 us
  starting transfers between devices: 32.2 us -> 24.5 us
  waiting for transfers between devices: 8.7 us -> 5.39 us
    another operation x10 -> x0, other arithmetic: 56.5 us -> none  [the longest x6 34 us: on_device(): factor_low = jnp.linalg.cholesky(gram_matrix)]
    dot_general x5 -> x0, matrix products: 18.8 us -> none  [the longest x1 4.3 us: on_device(): jnp.einsum('rs,sak->rak', row_place, products, precision=lax.Precision.HI...]
    pallas_call x0 -> x3, Pallas kernels: none -> 16.6 us  [the longest x1 11.1 us: next_basis(): pl.pallas_call(functools.partial(next_kernel, rows_total), out_shape=jax....]
    dot_general x2 -> x0, local copies, waits for them, and re-layouts: 10.2 us -> none  [the longest x1 5.09 us: on_device(): jnp.einsum('sab,sak->sbk', tiles, row_part, preferred_element_type=jnp.fl...]
    another operation x12 -> x0, local copies, waits for them, and re-layouts: 7.93 us -> none
    all_to_all x1 -> x0, starting transfers between devices: 6.72 us -> none  [from_everyone(): return lax.all_to_all(copies, axis, split_axis=0, concat_axis=0, tiled=True)]
    another operation x5 -> x0, matrix products: 6.49 us -> none  [the longest x3 4.34 us: on_device(): lax.linalg.triangular_solve(factor_low, local_y, left_side=False, lower=T...]
    gather x2 -> x0, local copies, waits for them, and re-layouts: 6.19 us -> none  [the longest x1 3.28 us: on_device(): blocks = stack[local_col]]
  transfers between devices with their start and end apart: 5 -> 4, of which waited for: 3 -> 2; matrix products, arithmetic and copies ran while one was open for 1% -> 0% of each run, Pallas kernels for 0% -> 0%
where the time goes in v1:
time: 107 us; the launch traced here: 106 us
  blocking collectives  54.6 us (51%)
  starting transfers between devices  24.5 us (23%)
  Pallas kernels  16.6 us (16%)
  waiting for transfers between devices  5.39 us (5%)
  local copies, waits for them, and re-layouts  4.29 us (4%)
    all_to_all x4, blocking collectives, exchange(): return lax.all_to_all(x, axes, split_axis=0, concat_axis=0, tiled=True)  54.6 us
    ppermute x1, starting transfers between devices, on_device(): above = lax.ppermute(lower, AXES, down)  12 us
    pallas_call x1, Pallas kernels, next_basis(): pl.pallas_call(functools.partial(next_kernel, rows_total), out_shape=jax....  11.1 us
    ppermute x1, starting transfers between devices, on_device(): high = lax.ppermute(q_block[:H * bs], AXES, down)  6.17 us
    pallas_call x1, Pallas kernels, band(): pl.pallas_call(functools.partial(band_kernel, nt), out_shape=(jax.ShapeDt...  5.06 us
    ppermute x1, starting transfers between devices, on_device(): low = lax.ppermute(q_block[rows - H * bs:], AXES, up)  4.49 us
    unnamed x8, local copies, waits for them, and re-layouts  4.24 us
    ppermute x1, waiting for transfers between devices, on_device(): high = lax.ppermute(q_block[:H * bs], AXES, down)  3.88 us
  transfers between devices with their start and end apart: 4, of which 2 were waited for; matrix products, arithmetic and copies ran while one was open for 0% of the time, Pallas kernels for 0%

profile of v1, /device:TPU:1, one launch (start us, length us, event | category | flops | bytes accessed | tf_op | source)
XLA Modules:
  0.0 106.2 jit_solution(11949203257425829894)
XLA Ops:
  0.0 4.5 %collective-permute-start = (bf16[1024,256]{1,0:T(8,128)(2,1)}, bf16[1024,256]{1,0:T(8,128)(2,1)S(1)}, u32[]{:S(2)}, u32[]{:S(2)}) collective-permute-start(bf16[1024,256]{1,0:T(8,128)(2,1)} %q_ref.1), channel_id=1, source_target_pairs={{0,1},{1,2},{2,3},{3,4},{4,5},{5,6},{6,7},{7,8},{8,9},{9,10},{10,1... | collective-permute-start | bytes 1572872 | tf_op jit(solution)/shard_map/ppermute | solution.py:243
  4.5 6.2 %collective-permute-start.1 = (bf16[1024,256]{1,0:T(8,128)(2,1)}, bf16[1024,256]{1,0:T(8,128)(2,1)S(1)}, u32[]{:S(2)}, u32[]{:S(2)}) collective-permute-start(bf16[1024,256]{1,0:T(8,128)(2,1)} %q_ref.1), channel_id=1, source_target_pairs={{1,0},{2,1},{3,2},{4,3},{5,4},{6,5},{7,6},{8,7},{9,8},{10,9},{11,1... | collective-permute-start | bytes 1572872 | tf_op jit(solution)/shard_map/ppermute | solution.py:244
  11.3 0.0 collective-permute-done.low_ref
  11.3 3.9 %collective-permute-done.1.high_ref = bf16[1024,256]{1,0:T(8,128)(2,1)S(1)} collective-permute-done((bf16[1024,256]{1,0:T(8,128)(2,1)}, bf16[1024,256]{1,0:T(8,128)(2,1)S(1)}, u32[]{:S(2)}, u32[]{:S(2)}) %collective-permute-start.1) | collective-permute-done | bytes 524320 | tf_op jit(solution)/shard_map/ppermute | solution.py:244
  15.2 0.0 copy-start
  15.2 1.9 %copy-done = bf16[6,512,512]{2,1,0:T(8,128)(2,1)S(1)} copy-done((bf16[6,512,512]{2,1,0:T(8,128)(2,1)S(1)}, bf16[6,512,512]{2,1,0:T(8,128)(2,1)}, u32[]{:S(2)}) %copy-start) | copy-done | bytes 3145752
  17.1 0.0 copy-start.1
  17.1 1.0 copy-done.1
  18.1 0.0 copy-start.2
  18.1 0.7 copy-done.2
  18.8 0.0 copy-start.3
  18.8 0.7 copy-done.3
  19.4 5.1 %band.1 = (f32[1024,256]{1,0:T(8,128)S(1)}, bf16[1024,256]{1,0:T(8,128)(2,1)S(1)}, bf16[1024,256]{1,0:T(8,128)(2,1)S(1)}) custom-call(s32[6]{0:T(128)S(1)} %copy-done.2, s32[6]{0:T(128)S(1)} %copy-done.3, s32[1]{0:T(128)S(6)} %copy.6.count_ref, bf16[6,512,512]{2,1,0:T(8,128)(2,1)S(1)} %copy-done, bf16[1024,256]{1,0:T(8,128)(2,1)S(1)} %collective-permute-done.low_ref, ...), custom_call_target="tpu_custom_call" | custom-call | flops 1610612736 | bytes 3145728 | tf_op jit(solution)/shard_map/band/pallas_call | solution.py:75
  24.5 1.9 %collective-permute-start.2 = (bf16[1024,256]{1,0:T(8,128)(2,1)S(1)}, bf16[1024,256]{1,0:T(8,128)(2,1)S(1)}, u32[]{:S(2)}, u32[]{:S(2)}) collective-permute-start(bf16[1024,256]{1,0:T(8,128)(2,1)S(1)} %get-tuple-element.11), channel_id=1, source_target_pairs={{0,1},{1,2},{2,3},{3,4},{4,5},{5,6},{6,7},{7,8},{8,9},{9,10},{10,1... | collective-permute-start | bytes 1572872 | tf_op jit(solution)/shard_map/ppermute | solution.py:248
  26.4 12.0 %collective-permute-start.3 = (bf16[1024,256]{1,0:T(8,128)(2,1)S(1)}, bf16[1024,256]{1,0:T(8,128)(2,1)S(1)}, u32[]{:S(2)}, u32[]{:S(2)}) collective-permute-start(bf16[1024,256]{1,0:T(8,128)(2,1)S(1)} %get-tuple-element.12), channel_id=1, source_target_pairs={{1,0},{2,1},{3,2},{4,3},{5,4},{6,5},{7,6},{8,7},{9,8},{10,9},{11,1... | collective-permute-start | bytes 1572872 | tf_op jit(solution)/shard_map/ppermute | solution.py:249
  38.4 0.0 collective-permute-done.2.below_ref
  38.4 1.5 %collective-permute-done.3.above_ref = bf16[1024,256]{1,0:T(8,128)(2,1)S(1)} collective-permute-done((bf16[1024,256]{1,0:T(8,128)(2,1)S(1)}, bf16[1024,256]{1,0:T(8,128)(2,1)S(1)}, u32[]{:S(2)}, u32[]{:S(2)}) %collective-permute-start.3) | collective-permute-done | bytes 524320 | tf_op jit(solution)/shard_map/ppermute | solution.py:249
  39.9 0.4 gram.1
  40.4 19.7 %all_to_all.20 = bf16[8,48,128]{2,1,0:T(8,128)(2,1)S(1)} all-to-all(bf16[8,48,128]{2,1,0:T(8,128)(2,1)S(1)} %bitcast.3), channel_id=1, replica_groups=mesh['grp'=8,'y'=8,'x'=4,'core'=2] {'x','core'}, dimensions={0} | all-to-all | bytes 196608 | tf_op jit(solution)/shard_map/all_to_all | solution.py:221
  60.1 9.8 %all_to_all.21 = bf16[8,48,128]{2,1,0:T(8,128)(2,1)S(1)} all-to-all(bf16[8,48,128]{2,1,0:T(8,128)(2,1)S(1)} %broadcast_in_dim.9), channel_id=1, replica_groups=mesh['grp'=8,'y'=8,'x'=4,'core'=2] {'y'}, dimensions={0} | all-to-all | bytes 196608 | tf_op jit(solution)/shard_map/all_to_all | solution.py:221
  70.0 14.2 %all_to_all.22 = bf16[8,48,128]{2,1,0:T(8,128)(2,1)S(1)} all-to-all(bf16[8,48,128]{2,1,0:T(8,128)(2,1)S(1)} %broadcast_in_dim.10), channel_id=1, replica_groups=mesh['grp'=8,'y'=8,'x'=4,'core'=2] {'grp'}, dimensions={0} | all-to-all | bytes 196608 | tf_op jit(solution)/shard_map/all_to_all | solution.py:221
  84.2 10.9 %all_to_all.23 = bf16[8,48,128]{2,1,0:T(8,128)(2,1)S(1)} all-to-all(bf16[8,48,128]{2,1,0:T(8,128)(2,1)S(1)} %broadcast_in_dim.11), channel_id=1, replica_groups=mesh['grp'=8,'y'=8,'x'=4,'core'=2] {'x','core'}, dimensions={0} | all-to-all | bytes 196608 | tf_op jit(solution)/shard_map/all_to_all | solution.py:221
  95.1 11.1 %next_basis.1 = f32[1024,256]{1,0:T(8,128)} custom-call(bf16[384,128]{1,0:T(8,128)(2,1)S(1)} %bitcast.2, f32[1024,256]{1,0:T(8,128)S(1)} %get-tuple-element.14.y_ref), custom_call_target="tpu_custom_call" | custom-call | flops 402653184 | bytes 2097152 | tf_op jit(solution)/shard_map/next_basis/pallas_call | solution.py:203
  (6 shorter events, 0.1 us)
Async XLA Ops:
  0.0 11.3 %collective-permute-start = (bf16[1024,256]{1,0:T(8,128)(2,1)}, bf16[1024,256]{1,0:T(8,128)(2,1)S(1)}, u32[]{:S(2)}, u32[]{:S(2)}) collective-permute-start(bf16[1024,256]{1,0:T(8,128)(2,1)} %q_ref.1), channel_id=1, source_target_pairs={{0,1},{1,2},{2,3},{3,4},{4,5},{5,6},{6,7},{7,8},{8,9},{9,10},{10,1... | collective-permute-start | bytes 1572872 | tf_op jit(solution)/shard_map/ppermute | solution.py:243
  4.5 10.7 %collective-permute-start.1 = (bf16[1024,256]{1,0:T(8,128)(2,1)}, bf16[1024,256]{1,0:T(8,128)(2,1)S(1)}, u32[]{:S(2)}, u32[]{:S(2)}) collective-permute-start(bf16[1024,256]{1,0:T(8,128)(2,1)} %q_ref.1), channel_id=1, source_target_pairs={{1,0},{2,1},{3,2},{4,3},{5,4},{6,5},{7,6},{8,7},{9,8},{10,9},{11,1... | collective-permute-start | bytes 1572872 | tf_op jit(solution)/shard_map/ppermute | solution.py:244
  15.2 1.9 %copy-start = (bf16[6,512,512]{2,1,0:T(8,128)(2,1)S(1)}, bf16[6,512,512]{2,1,0:T(8,128)(2,1)}, u32[]{:S(2)}) copy-start(bf16[6,512,512]{2,1,0:T(8,128)(2,1)} %tiles_ref.1) | copy-start | bytes 9437188
  17.1 1.0 copy-start.1
  18.1 0.7 copy-start.2
  18.8 0.7 copy-start.3
  24.5 13.9 %collective-permute-start.2 = (bf16[1024,256]{1,0:T(8,128)(2,1)S(1)}, bf16[1024,256]{1,0:T(8,128)(2,1)S(1)}, u32[]{:S(2)}, u32[]{:S(2)}) collective-permute-start(bf16[1024,256]{1,0:T(8,128)(2,1)S(1)} %get-tuple-element.11), channel_id=1, source_target_pairs={{0,1},{1,2},{2,3},{3,4},{4,5},{5,6},{6,7},{7,8},{8,9},{9,10},{10,1... | collective-permute-start | bytes 1572872 | tf_op jit(solution)/shard_map/ppermute | solution.py:248
  26.4 13.5 %collective-permute-start.3 = (bf16[1024,256]{1,0:T(8,128)(2,1)S(1)}, bf16[1024,256]{1,0:T(8,128)(2,1)S(1)}, u32[]{:S(2)}, u32[]{:S(2)}) collective-permute-start(bf16[1024,256]{1,0:T(8,128)(2,1)S(1)} %get-tuple-element.12), channel_id=1, source_target_pairs={{1,0},{2,1},{3,2},{4,3},{5,4},{6,5},{7,6},{8,7},{9,8},{10,9},{11,1... | collective-permute-start | bytes 1572872 | tf_op jit(solution)/shard_map/ppermute | solution.py:249

commit v2 on v1

v2 whole, which is shorter than its diff:
```python
import functools

import jax
import jax.numpy as jnp
from jax import lax
from jax.experimental import pallas as pl
from jax.experimental.pallas import tpu as pltpu
from jax.sharding import Mesh
from jax.sharding import PartitionSpec as P

H = 2
LEAF = 64
AXES = ("grp", "y", "x", "core")
F32 = jnp.float32
BF16 = jnp.bfloat16


def dot(a, b, ca, cb):
    return lax.dot_general(a, b, (((ca,), (cb,)), ((), ())), preferred_element_type=F32)


SMEM = pl.BlockSpec(memory_space=pltpu.SMEM)
VMEM = pl.BlockSpec(memory_space=pltpu.VMEM)
HBM = pl.BlockSpec(memory_space=pltpu.HBM)


class Slots:
    def __init__(self, table, slots, own, nt):
        self.table, self.slots, self.own, self.nt = table, slots, own, nt
        self.odd = lax.rem(lax.div(table[0], own), 2) == 1

    def live(self, s):
        return s < self.table[2 * self.slots]

    def row(self, s):
        return lax.rem(self.table[s], self.own)

    def column(self, s):
        off = self.table[self.slots + s] - self.table[s] + H
        off = jnp.where(off < 0, off + self.nt, off)
        off = jnp.where(off >= self.nt, off - self.nt, off)
        return self.row(s) + off

    def is_own(self, s):
        column = self.column(s)
        return jnp.logical_and(column >= H, column < H + self.own)

    def is_across(self, s):
        column = self.column(s)
        return jnp.where(self.odd, column >= H + self.own, column < H)

    def is_beside(self, s):
        column = self.column(s)
        return jnp.where(self.odd, column < H, column >= H + self.own)

    def in_side(self, s):
        column = self.column(s)
        return jnp.where(column < H, column, column - H - self.own)

    def in_own(self, s):
        return self.column(s) - H


def own_kernel(nt, table, tiles_ref, q_ref, held_ref, acc_ref, q_held, sems):
    slots = held_ref.shape[0]
    own = acc_ref.shape[0]
    at = Slots(table, slots, own, nt)
    copies = [pltpu.make_async_copy(q_ref, q_held, sems.at[slots])]
    copies += [
        pltpu.make_async_copy(tiles_ref.at[s], held_ref.at[s], sems.at[s]) for s in range(slots)
    ]
    for copy in copies:
        copy.start()
    acc_ref[...] = jnp.zeros_like(acc_ref)
    copies[0].wait()
    for s in range(slots):
        copies[s + 1].wait()

        @pl.when(jnp.logical_and(at.live(s), at.is_own(s)))
        def _():
            acc_ref[at.row(s)] += dot(held_ref[s], q_held[at.in_own(s)], 1, 0)


def across_kernel(nt, table, held_ref, acc_in, across_ref, beside_ref, aq_ref, out_ref, acc, terms):
    slots = held_ref.shape[0]
    at = Slots(table, slots, acc.shape[0], nt)
    acc[...] = acc_in[...]
    terms[...] = jnp.zeros_like(terms)
    for s in range(slots):
        for there, side in ((at.is_beside(s), beside_ref), (at.is_across(s), across_ref)):

            @pl.when(jnp.logical_and(at.live(s), there))
            def _(side=side):
                acc[at.row(s)] += dot(held_ref[s], side[at.in_side(s)], 1, 0)

    aq_ref[...] = acc[...].astype(BF16)
    for s in range(slots):

        @pl.when(jnp.logical_and(at.live(s), at.is_across(s)))
        def _():
            terms[at.in_side(s)] += dot(held_ref[s], aq_ref[at.row(s)], 0, 0)

    out_ref[...] = terms[...].astype(BF16)


def rest_kernel(nt, table, held_ref, aq_ref, out_ref, own_ref, terms):
    slots = held_ref.shape[0]
    at = Slots(table, slots, own_ref.shape[0], nt)
    terms[...] = jnp.zeros_like(terms)
    own_ref[...] = jnp.zeros_like(own_ref)
    for s in range(slots):
        for there, sums, place in (
            (at.is_beside(s), terms, at.in_side(s)),
            (at.is_own(s), own_ref, at.in_own(s)),
        ):

            @pl.when(jnp.logical_and(at.live(s), there))
            def _(sums=sums, place=place):
                sums[place] += dot(held_ref[s], aq_ref[at.row(s)], 0, 0)

    out_ref[...] = terms[...].astype(BF16)


def kernel_call(body, outs, ins, scratch, products, args):
    bs = args[1].shape[-1]
    flops = 2 * products * bs * bs * outs[-1].shape[-1]
    return pl.pallas_call(
        body,
        out_shape=tuple(outs),
        in_specs=ins,
        out_specs=(VMEM,) * len(outs),
        scratch_shapes=scratch,
        compiler_params=pltpu.CompilerParams(vmem_limit_bytes=24 << 20),
        cost_estimate=pl.CostEstimate(flops=flops, bytes_accessed=4 << 20, transcendentals=0),
    )(*args)


def exchanged(x, pairs, shape):
    return lax.ppermute(x, AXES, pairs).reshape(shape)


def band(tiles, tile_row, tile_col, tile_count, q):
    slots, bs, _ = tiles.shape
    rows, k = q.shape
    own = rows // bs
    peers = lax.axis_size(AXES)
    nt = own * peers
    beside = [(d, d + 1 - 2 * (d % 2)) for d in range(peers)]
    across = [(d, (d - 1 + 2 * (d % 2)) % peers) for d in range(peers)]
    side = (H, bs, k)
    held = jax.ShapeDtypeStruct(tiles.shape, BF16)
    sums = jax.ShapeDtypeStruct((own, bs, k), F32)
    rim = jax.ShapeDtypeStruct(side, BF16)
    table = jnp.concatenate([tile_row, tile_col, tile_count])
    q_across = exchanged(q, across, side)
    q_beside = exchanged(q, beside, side)
    held, acc = kernel_call(
        functools.partial(own_kernel, nt), [held, sums], [SMEM, HBM, HBM],
        [pltpu.VMEM((own, bs, k), BF16), pltpu.SemaphoreType.DMA((slots + 1,))],
        slots, (table, tiles, q.reshape(own, bs, k)),
    )
    aq, rim_across = kernel_call(
        functools.partial(across_kernel, nt),
        [jax.ShapeDtypeStruct((own, bs, k), BF16), rim], [SMEM] + [VMEM] * 4,
        [pltpu.VMEM((own, bs, k), F32), pltpu.VMEM(side, F32)],
        2 * slots, (table, held, acc, q_across, q_beside),
    )
    from_across = exchanged(rim_across, across, (rows, k))
    rim_beside, sums = kernel_call(
        functools.partial(rest_kernel, nt), [rim, sums], [SMEM] + [VMEM] * 2,
        [pltpu.VMEM(side, F32)],
        slots, (table, held, aq),
    )
    from_beside = exchanged(rim_beside, beside, (rows, k))
    return sums.reshape(rows, k), from_across, from_beside


def gram_kernel(own_ref, below_ref, above_ref, y_ref, gram_ref):
    y = own_ref[...] + below_ref[...].astype(F32) + above_ref[...].astype(F32)
    y_ref[...] = y
    b = y.astype(BF16)
    half = b.shape[1] // 2
    full = dot(b, b, 0, 0)
    gram_ref[0:half, :] = full[:half, :half].astype(BF16)
    gram_ref[half : 2 * half, :] = full[:half, half:].astype(BF16)
    gram_ref[2 * half :, :] = full[half:, half:].astype(BF16)


def gram(own, below, above):
    rows, k = own.shape
    vmem = pl.BlockSpec(memory_space=pltpu.VMEM)
    return pl.pallas_call(
        gram_kernel,
        out_shape=(
            jax.ShapeDtypeStruct((rows, k), F32),
            jax.ShapeDtypeStruct((3 * k // 2, k // 2), BF16),
        ),
        in_specs=[vmem] * 3,
        out_specs=(vmem,) * 2,
        compiler_params=pltpu.CompilerParams(vmem_limit_bytes=32 << 20),
        cost_estimate=pl.CostEstimate(
            flops=2 * rows * k * k, bytes_accessed=8 * rows * k, transcendentals=0
        ),
        name="gram",
    )(own, below, above)


def spread(piece):
    return jnp.broadcast_to(piece, (8, 128))


def leaf_inverse(d, zero):
    n = d.shape[0]
    pieces = n // 8
    eye = (
        lax.broadcasted_iota(jnp.int32, (n, n), 0) == lax.broadcasted_iota(jnp.int32, (n, n), 1)
    ).astype(F32)
    both = jnp.concatenate([eye, d], axis=1)
    a = [both[8 * r : 8 * r + 8, :] for r in range(pieces)]
    line = lax.broadcasted_iota(jnp.int32, (8, 128), 0)
    for t in range(pieces):
        cols = [
            [spread(a[r][:, n + 8 * t + i : n + 8 * t + i + 1]) for r in range(t, pieces)]
            for i in range(8)
        ]
        for col in cols:
            col[0] = col[0] + zero
        pivot = spread(cols[0][0][0:1, :])
        roots = jnp.ones((8, 128), F32)
        for i in range(8):
            root = lax.rsqrt(pivot)
            roots = jnp.where(line == i, root, roots)
            if i < 7:
                beside = spread(cols[i][0][i + 1 : i + 2, :]) * root
                pivot = spread(cols[i + 1][0][i + 1 : i + 2, :]) - beside * beside
            by = [c * root for c in cols[i]]
            for j in range(i + 1, 8):
                row = spread(cols[j][0][i : i + 1, :]) * root
                cols[j] = [c - b * row for c, b in zip(cols[j], by)]
            by[0] = jnp.where(line > i, by[0], 0.0)
            row = spread(a[t][i : i + 1, :]) * root
            for r, b in enumerate(by):
                a[t + r] = a[t + r] - b * row
        a[t] = a[t] * roots
    return jnp.concatenate([piece[:, :n] for piece in a], axis=0)


def split(x):
    hi = x.astype(BF16)
    return hi, (x - hi.astype(F32)).astype(BF16)


def dot3(a, b, ca, cb):
    a_hi, a_lo = split(a)
    b_hi, b_lo = split(b)
    return dot(a_hi, b_hi, ca, cb) + (dot(a_lo, b_hi, ca, cb) + dot(a_hi, b_lo, ca, cb))


def factor_inverse(g, zero):
    g11, g12, g22 = g
    x11 = whole_inverse(g11, zero)
    b = dot3(x11, g12, 1, 0)
    s = g22 - dot3(b, b, 0, 0)
    x22 = whole_inverse(s, zero)
    x21 = -dot3(x22, dot3(b, x11, 0, 0), 1, 0)
    return x11, x21, x22


def joined(x11, x21, x22):
    upper = jnp.concatenate([x11, jnp.zeros_like(x11)], axis=1)
    return jnp.concatenate([upper, jnp.concatenate([x21, x22], axis=1)], axis=0)


def whole_inverse(d, zero):
    n = d.shape[0]
    if n == LEAF:
        return leaf_inverse(d, zero)
    h = n // 2
    return joined(*factor_inverse((d[:h, :h], d[:h, h:], d[h:, h:]), zero))


def next_kernel(rows_total, gram_ref, y_ref, out_ref):
    half = gram_ref.shape[1]
    g = [gram_ref[pl.ds(i * half, half), :].astype(F32) / rows_total for i in range(3)]
    x = joined(*factor_inverse(g, y_ref[0:8, 0:128] * 0.0))
    out_ref[...] = dot3(y_ref[...], x, 1, 1)


def next_basis(rows_total, packed, y):
    rows, k = y.shape
    vmem = pl.BlockSpec(memory_space=pltpu.VMEM)
    return pl.pallas_call(
        functools.partial(next_kernel, rows_total),
        out_shape=jax.ShapeDtypeStruct((rows, k), F32),
        in_specs=[vmem] * 2,
        out_specs=vmem,
        compiler_params=pltpu.CompilerParams(vmem_limit_bytes=32 << 20),
        cost_estimate=pl.CostEstimate(
            flops=6 * rows * k * k, bytes_accessed=8 * rows * k, transcendentals=0
        ),
        name="next_basis",
    )(packed, y)


def summed(x):
    return x.astype(F32).sum(axis=0).astype(BF16)


def exchange(x, axes):
    return lax.all_to_all(x, axes, split_axis=0, concat_axis=0, tiled=True)


def from_everyone(x, axes):
    return exchange(jnp.broadcast_to(x, (lax.axis_size(axes), *x.shape)), axes)


def sum_everywhere(x):
    near = ("x", "core")
    parts = x.reshape(lax.axis_size(near), -1, x.shape[1])
    own = summed(exchange(parts, near))
    own = summed(from_everyone(own, "y"))
    own = summed(from_everyone(own, "grp"))
    return from_everyone(own, near).reshape(x.shape)


def on_device(tiles, tile_row, tile_col, tile_count, q_block):
    rows_total = q_block.shape[0] * lax.axis_size(AXES)
    y, packed = gram(*band(tiles, tile_row, tile_col, tile_count, q_block))
    return next_basis(rows_total, sum_everywhere(packed), y)


def solution(mesh):
    torus = Mesh(mesh.devices.reshape(mesh.shape["grp"], 8, 4, 2), AXES)
    return jax.shard_map(
        on_device,
        mesh=torus,
        in_specs=(P(AXES, None, None), P(AXES), P(AXES), P(AXES), P(AXES, None)),
        out_specs=P(AXES, None),
        check_vma=False,
    )
```

time: 107 us -> 101 us (0.944)
  blocking collectives: 54.6 us -> 46.9 us
  waiting for transfers between devices: 5.39 us -> 12 us
  Pallas kernels: 16.6 us -> 13.9 us
  starting transfers between devices: 24.5 us -> 23 us
  local copies, waits for them, and re-layouts: 4.29 us -> 2.98 us
    all_to_all x4, blocking collectives: 54.6 us -> 46.9 us  [exchange(): return lax.all_to_all(x, axes, split_axis=0, concat_axis=0, tiled=True)]
    ppermute x4, waiting for transfers between devices: 5.39 us -> 12 us  [exchanged(): return lax.ppermute(x, AXES, pairs).reshape(shape)]
    pallas_call x1, Pallas kernels: 11.1 us -> 8.78 us  [next_basis(): pl.pallas_call(functools.partial(next_kernel, rows_total), out_shape=jax....]
    ppermute x4, starting transfers between devices: 24.5 us -> 23 us  [exchanged(): return lax.ppermute(x, AXES, pairs).reshape(shape)]
    unnamed x8 -> x4, local copies, waits for them, and re-layouts: 4.24 us -> 2.93 us
    pallas_call x1 -> x3, Pallas kernels: 5.06 us -> 4.78 us  [kernel_call(): pl.pallas_call(body, out_shape=tuple(outs), in_specs=ins, out_specs=(VMEM...]
  transfers between devices with their start and end apart: 4 -> 4, of which waited for: 2 -> 2; matrix products, arithmetic and copies ran while one was open for 0% -> 1% of each run, Pallas kernels for 0% -> 1%
where the time goes in v2:
time: 101 us; the launch traced here: 100 us
  blocking collectives  46.9 us (46%)
  starting transfers between devices  23 us (23%)
  Pallas kernels  13.9 us (14%)
  waiting for transfers between devices  12 us (12%)
  local copies, waits for them, and re-layouts  2.98 us (3%)
    all_to_all x4, blocking collectives, exchange(): return lax.all_to_all(x, axes, split_axis=0, concat_axis=0, tiled=True)  46.9 us
    ppermute x4, starting transfers between devices, exchanged(): return lax.ppermute(x, AXES, pairs).reshape(shape)  23 us
    ppermute x4, waiting for transfers between devices, exchanged(): return lax.ppermute(x, AXES, pairs).reshape(shape)  12 us
    pallas_call x1, Pallas kernels, next_basis(): pl.pallas_call(functools.partial(next_kernel, rows_total), out_shape=jax....  8.78 us
    pallas_call x3, Pallas kernels, kernel_call(): pl.pallas_call(body, out_shape=tuple(outs), in_specs=ins, out_specs=(VMEM...  4.78 us
    unnamed x4, local copies, waits for them, and re-layouts  2.93 us
  transfers between devices with their start and end apart: 4, of which 2 were waited for; matrix products, arithmetic and copies ran while one was open for 1% of the time, Pallas kernels for 1%

profile of v2, /device:TPU:1, one launch (start us, length us, event | category | flops | bytes accessed | tf_op | source)
XLA Modules:
  0.0 100.4 jit_solution(11920798707432624463)
XLA Ops:
  0.0 8.7 %collective-permute-start.1 = (bf16[1024,256]{1,0:T(8,128)(2,1)}, bf16[1024,256]{1,0:T(8,128)(2,1)S(1)}, u32[]{:S(2)}, u32[]{:S(2)}) collective-permute-start(bf16[1024,256]{1,0:T(8,128)(2,1)} %param.9), channel_id=1, source_target_pairs={{0,1},{1,0},{2,3},{3,2},{4,5},{5,4},{6,7},{7,6},{8,9},{9,8},{10,11... | collective-permute-start | bytes 1572872 | tf_op jit(solution)/shard_map/ppermute | solution.py:139
  8.7 1.9 %collective-permute-start = (bf16[1024,256]{1,0:T(8,128)(2,1)}, bf16[1024,256]{1,0:T(8,128)(2,1)S(1)}, u32[]{:S(2)}, u32[]{:S(2)}) collective-permute-start(bf16[1024,256]{1,0:T(8,128)(2,1)} %param.9), channel_id=1, source_target_pairs={{0,511},{1,2},{2,1},{3,4},{4,3},{5,6},{6,5},{7,8},{8,7},{9,10},{10... | collective-permute-start | bytes 1572872 | tf_op jit(solution)/shard_map/ppermute | solution.py:139
  11.3 0.7 pad_add_fusion.table
  12.1 0.0 copy-start
  12.1 1.9 %copy-done = bf16[6,512,512]{2,1,0:T(8,128)(2,1)S(1)} copy-done((bf16[6,512,512]{2,1,0:T(8,128)(2,1)S(1)}, bf16[6,512,512]{2,1,0:T(8,128)(2,1)}, u32[]{:S(2)}) %copy-start) | copy-done | bytes 3145752
  14.0 0.0 copy-start.1
  14.0 1.0 %copy-done.1 = bf16[1024,256]{1,0:T(8,128)(2,1)S(1)} copy-done((bf16[1024,256]{1,0:T(8,128)(2,1)S(1)}, bf16[1024,256]{1,0:T(8,128)(2,1)}, u32[]{:S(2)}) %copy-start.1) | copy-done | bytes 524312
  15.0 1.3 %shard_map.55 = (bf16[6,512,512]{2,1,0:T(8,128)(2,1)S(1)}, f32[2,512,256]{2,1,0:T(8,128)S(1)}) custom-call(s32[13]{0:T(128)S(1)} %pad_add_fusion.table, bf16[6,512,512]{2,1,0:T(8,128)(2,1)S(1)} %copy-done, bf16[2,512,256]{2,1,0:T(8,128)(2,1)S(1)} %bitcast.9), custom_call_target="tpu_custom_call" | custom-call | flops 805306368 | bytes 4194304 | tf_op jit(solution)/shard_map/pallas_call | solution.py:127
  16.3 0.0 collective-permute-done.1
  16.3 3.1 %collective-permute-done = bf16[1024,256]{1,0:T(8,128)(2,1)S(1)} collective-permute-done((bf16[1024,256]{1,0:T(8,128)(2,1)}, bf16[1024,256]{1,0:T(8,128)(2,1)S(1)}, u32[]{:S(2)}, u32[]{:S(2)}) %collective-permute-start) | collective-permute-done | bytes 524320 | tf_op jit(solution)/shard_map/ppermute | solution.py:139
  19.5 1.9 %shard_map.56 = (bf16[2,512,256]{2,1,0:T(8,128)(2,1)S(1)}, bf16[2,512,256]{2,1,0:T(8,128)(2,1)S(1)}) custom-call(s32[13]{0:T(128)S(1)} %pad_add_fusion.table, bf16[6,512,512]{2,1,0:T(8,128)(2,1)S(1)} %get-tuple-element.13.held_ref, f32[2,512,256]{2,1,0:T(8,128)S(1)} %get-tuple-element.14.acc_in, bf16[2,512,256]{2,1,0:T(8,128)(2,1)S(1)} %bitcast.15, ...), custom_call_target="tpu_custom_call" | custom-call | flops 1610612736 | bytes 4194304 | tf_op jit(solution)/shard_map/pallas_call | solution.py:127
  21.4 1.5 %shard_map.57 = (bf16[2,512,256]{2,1,0:T(8,128)(2,1)S(1)}, f32[2,512,256]{2,1,0:T(8,128)S(1)}) custom-call(s32[13]{0:T(128)S(1)} %pad_add_fusion.table, bf16[6,512,512]{2,1,0:T(8,128)(2,1)S(1)} %get-tuple-element.13.held_ref, bf16[2,512,256]{2,1,0:T(8,128)(2,1)S(1)} %get-tuple-element.15.aq_ref), custom_call_target="tpu_custom_call" | custom-call | flops 805306368 | bytes 4194304 | tf_op jit(solution)/shard_map/pallas_call | solution.py:127
  22.9 10.4 %collective-permute-start.3 = (bf16[2,512,256]{2,1,0:T(8,128)(2,1)S(1)}, bf16[2,512,256]{2,1,0:T(8,128)(2,1)S(1)}, u32[]{:S(2)}, u32[]{:S(2)}) collective-permute-start(bf16[2,512,256]{2,1,0:T(8,128)(2,1)S(1)} %get-tuple-element.18), channel_id=1, source_target_pairs={{0,1},{1,0},{2,3},{3,2},{4,5},{5,4},{6,7},{7,6},{8,9},{9,8},{10,11... | collective-permute-start | bytes 1572872 | tf_op jit(solution)/shard_map/ppermute | solution.py:139
  33.4 1.9 %collective-permute-start.2 = (bf16[2,512,256]{2,1,0:T(8,128)(2,1)S(1)}, bf16[2,512,256]{2,1,0:T(8,128)(2,1)S(1)}, u32[]{:S(2)}, u32[]{:S(2)}) collective-permute-start(bf16[2,512,256]{2,1,0:T(8,128)(2,1)S(1)} %get-tuple-element.17), channel_id=1, source_target_pairs={{0,511},{1,2},{2,1},{3,4},{4,3},{5,6},{6,5},{7,8},{8,7},{9,10},{10... | collective-permute-start | bytes 1572872 | tf_op jit(solution)/shard_map/ppermute | solution.py:139
  35.3 0.0 collective-permute-done.3
  35.3 8.9 %collective-permute-done.2 = bf16[2,512,256]{2,1,0:T(8,128)(2,1)S(1)} collective-permute-done((bf16[2,512,256]{2,1,0:T(8,128)(2,1)S(1)}, bf16[2,512,256]{2,1,0:T(8,128)(2,1)S(1)}, u32[]{:S(2)}, u32[]{:S(2)}) %collective-permute-start.2) | collective-permute-done | bytes 524320 | tf_op jit(solution)/shard_map/ppermute | solution.py:139
  44.2 0.4 gram.1
  44.6 12.5 %all_to_all.20 = bf16[8,48,128]{2,1,0:T(8,128)(2,1)S(1)} all-to-all(bf16[8,48,128]{2,1,0:T(8,128)(2,1)S(1)} %bitcast.13), channel_id=1, replica_groups=mesh['grp'=8,'y'=8,'x'=4,'core'=2] {'x','core'}, dimensions={0} | all-to-all | bytes 196608 | tf_op jit(solution)/shard_map/all_to_all | solution.py:310
  57.1 10.0 %all_to_all.21 = bf16[8,48,128]{2,1,0:T(8,128)(2,1)S(1)} all-to-all(bf16[8,48,128]{2,1,0:T(8,128)(2,1)S(1)} %broadcast_in_dim.9), channel_id=1, replica_groups=mesh['grp'=8,'y'=8,'x'=4,'core'=2] {'y'}, dimensions={0} | all-to-all | bytes 196608 | tf_op jit(solution)/shard_map/all_to_all | solution.py:310
  67.2 13.5 %all_to_all.22 = bf16[8,48,128]{2,1,0:T(8,128)(2,1)S(1)} all-to-all(bf16[8,48,128]{2,1,0:T(8,128)(2,1)S(1)} %broadcast_in_dim.10), channel_id=1, replica_groups=mesh['grp'=8,'y'=8,'x'=4,'core'=2] {'grp'}, dimensions={0} | all-to-all | bytes 196608 | tf_op jit(solution)/shard_map/all_to_all | solution.py:310
  80.7 10.9 %all_to_all.23 = bf16[8,48,128]{2,1,0:T(8,128)(2,1)S(1)} all-to-all(bf16[8,48,128]{2,1,0:T(8,128)(2,1)S(1)} %broadcast_in_dim.11), channel_id=1, replica_groups=mesh['grp'=8,'y'=8,'x'=4,'core'=2] {'x','core'}, dimensions={0} | all-to-all | bytes 196608 | tf_op jit(solution)/shard_map/all_to_all | solution.py:310
  91.6 8.8 %next_basis.1 = f32[1024,256]{1,0:T(8,128)} custom-call(bf16[384,128]{1,0:T(8,128)(2,1)S(1)} %bitcast.12, f32[1024,256]{1,0:T(8,128)S(1)} %get-tuple-element.20.y_ref), custom_call_target="tpu_custom_call" | custom-call | flops 402653184 | bytes 2097152 | tf_op jit(solution)/shard_map/next_basis/pallas_call | solution.py:292
  (6 shorter events, 0.1 us)
Async XLA Ops:
  0.0 16.3 %collective-permute-start.1 = (bf16[1024,256]{1,0:T(8,128)(2,1)}, bf16[1024,256]{1,0:T(8,128)(2,1)S(1)}, u32[]{:S(2)}, u32[]{:S(2)}) collective-permute-start(bf16[1024,256]{1,0:T(8,128)(2,1)} %param.9), channel_id=1, source_target_pairs={{0,1},{1,0},{2,3},{3,2},{4,5},{5,4},{6,7},{7,6},{8,9},{9,8},{10,11... | collective-permute-start | bytes 1572872 | tf_op jit(solution)/shard_map/ppermute | solution.py:139
  8.7 10.7 %collective-permute-start = (bf16[1024,256]{1,0:T(8,128)(2,1)}, bf16[1024,256]{1,0:T(8,128)(2,1)S(1)}, u32[]{:S(2)}, u32[]{:S(2)}) collective-permute-start(bf16[1024,256]{1,0:T(8,128)(2,1)} %param.9), channel_id=1, source_target_pairs={{0,511},{1,2},{2,1},{3,4},{4,3},{5,6},{6,5},{7,8},{8,7},{9,10},{10... | collective-permute-start | bytes 1572872 | tf_op jit(solution)/shard_map/ppermute | solution.py:139
  12.1 1.9 %copy-start = (bf16[6,512,512]{2,1,0:T(8,128)(2,1)S(1)}, bf16[6,512,512]{2,1,0:T(8,128)(2,1)}, u32[]{:S(2)}) copy-start(bf16[6,512,512]{2,1,0:T(8,128)(2,1)} %tiles_ref.1) | copy-start | bytes 9437188
  14.0 1.0 %copy-start.1 = (bf16[1024,256]{1,0:T(8,128)(2,1)S(1)}, bf16[1024,256]{1,0:T(8,128)(2,1)}, u32[]{:S(2)}) copy-start(bf16[1024,256]{1,0:T(8,128)(2,1)} %param.9) | copy-start | bytes 1572868
  22.9 12.4 %collective-permute-start.3 = (bf16[2,512,256]{2,1,0:T(8,128)(2,1)S(1)}, bf16[2,512,256]{2,1,0:T(8,128)(2,1)S(1)}, u32[]{:S(2)}, u32[]{:S(2)}) collective-permute-start(bf16[2,512,256]{2,1,0:T(8,128)(2,1)S(1)} %get-tuple-element.18), channel_id=1, source_target_pairs={{0,1},{1,0},{2,3},{3,2},{4,5},{5,4},{6,7},{7,6},{8,9},{9,8},{10,11... | collective-permute-start | bytes 1572872 | tf_op jit(solution)/shard_map/ppermute | solution.py:139
  33.4 10.8 %collective-permute-start.2 = (bf16[2,512,256]{2,1,0:T(8,128)(2,1)S(1)}, bf16[2,512,256]{2,1,0:T(8,128)(2,1)S(1)}, u32[]{:S(2)}, u32[]{:S(2)}) collective-permute-start(bf16[2,512,256]{2,1,0:T(8,128)(2,1)S(1)} %get-tuple-element.17), channel_id=1, source_target_pairs={{0,511},{1,2},{2,1},{3,4},{4,3},{5,6},{6,5},{7,8},{8,7},{9,10},{10... | collective-permute-start | bytes 1572872 | tf_op jit(solution)/shard_map/ppermute | solution.py:139

commit v3 on v2

--- a/solution.py
+++ b/solution.py
@@ -10,7 +10,8 @@
 
 H = 2
 LEAF = 64
-AXES = ("grp", "y", "x", "core")
+WIDTH = 16
+AXES = ("z_high", "z_low", "y", "x", "core")
 F32 = jnp.float32
 BF16 = jnp.bfloat16
 
@@ -61,7 +62,7 @@
         return self.column(s) - H
 
 
-def own_kernel(nt, table, tiles_ref, q_ref, held_ref, acc_ref, q_held, sems):
+def near_kernel(nt, table, tiles_ref, q_ref, beside_ref, held_ref, acc_ref, q_held, sems):
     slots = held_ref.shape[0]
     own = acc_ref.shape[0]
     at = Slots(table, slots, own, nt)
@@ -75,23 +76,26 @@
     copies[0].wait()
     for s in range(slots):
         copies[s + 1].wait()
-
-        @pl.when(jnp.logical_and(at.live(s), at.is_own(s)))
-        def _():
-            acc_ref[at.row(s)] += dot(held_ref[s], q_held[at.in_own(s)], 1, 0)
-
-
-def across_kernel(nt, table, held_ref, acc_in, across_ref, beside_ref, aq_ref, out_ref, acc, terms):
+        for there, side, place in (
+            (at.is_own(s), q_held, at.in_own(s)),
+            (at.is_beside(s), beside_ref, at.in_side(s)),
+        ):
+
+            @pl.when(jnp.logical_and(at.live(s), there))
+            def _(side=side, place=place):
+                acc_ref[at.row(s)] += dot(held_ref[s], side[place], 1, 0)
+
+
+def across_kernel(nt, table, held_ref, acc_in, across_ref, aq_ref, out_ref, acc, terms):
     slots = held_ref.shape[0]
     at = Slots(table, slots, acc.shape[0], nt)
     acc[...] = acc_in[...]
     terms[...] = jnp.zeros_like(terms)
     for s in range(slots):
-        for there, side in ((at.is_beside(s), beside_ref), (at.is_across(s), across_ref)):
-
-            @pl.when(jnp.logical_and(at.live(s), there))
-            def _(side=side):
-                acc[at.row(s)] += dot(held_ref[s], side[at.in_side(s)], 1, 0)
+
+        @pl.when(jnp.logical_and(at.live(s), at.is_across(s)))
+        def _():
+            acc[at.row(s)] += dot(held_ref[s], across_ref[at.in_side(s)], 1, 0)
 
     aq_ref[...] = acc[...].astype(BF16)
     for s in range(slots):
@@ -133,6 +137,10 @@
         compiler_params=pltpu.CompilerParams(vmem_limit_bytes=24 << 20),
         cost_estimate=pl.CostEstimate(flops=flops, bytes_accessed=4 << 20, transcendentals=0),
     )(*args)
+
+
+def in_hbm(x):
+    return pltpu.with_memory_space_constraint(x, pltpu.HBM)
 
 
 def exchanged(x, pairs, shape):
@@ -155,15 +163,15 @@
     q_across = exchanged(q, across, side)
     q_beside = exchanged(q, beside, side)
     held, acc = kernel_call(
-        functools.partial(own_kernel, nt), [held, sums], [SMEM, HBM, HBM],
+        functools.partial(near_kernel, nt), [held, sums], [SMEM, HBM, HBM, VMEM],
         [pltpu.VMEM((own, bs, k), BF16), pltpu.SemaphoreType.DMA((slots + 1,))],
-        slots, (table, tiles, q.reshape(own, bs, k)),
+        slots, (table, in_hbm(tiles), in_hbm(q.reshape(own, bs, k)), q_beside),
     )
     aq, rim_across = kernel_call(
         functools.partial(across_kernel, nt),
-        [jax.ShapeDtypeStruct((own, bs, k), BF16), rim], [SMEM] + [VMEM] * 4,
+        [jax.ShapeDtypeStruct((own, bs, k), BF16), rim], [SMEM] + [VMEM] * 3,
         [pltpu.VMEM((own, bs, k), F32), pltpu.VMEM(side, F32)],
-        2 * slots, (table, held, acc, q_across, q_beside),
+        slots, (table, held, acc, q_across),
     )
     from_across = exchanged(rim_across, across, (rows, k))
     rim_beside, sums = kernel_call(
@@ -218,30 +226,34 @@
     both = jnp.concatenate([eye, d], axis=1)
     a = [both[8 * r : 8 * r + 8, :] for r in range(pieces)]
     line = lax.broadcasted_iota(jnp.int32, (8, 128), 0)
-    for t in range(pieces):
+    for first in range(0, n, WIDTH):
+        top = first // 8
         cols = [
-            [spread(a[r][:, n + 8 * t + i : n + 8 * t + i + 1]) for r in range(t, pieces)]
-            for i in range(8)
+            [spread(a[r][:, n + first + i : n + first + i + 1]) for r in range(top, pieces)]
+            for i in range(WIDTH)
         ]
         for col in cols:
             col[0] = col[0] + zero
         pivot = spread(cols[0][0][0:1, :])
-        roots = jnp.ones((8, 128), F32)
-        for i in range(8):
+        roots = None
+        for i in range(WIDTH):
+            at, k = divmod(i, 8)
             root = lax.rsqrt(pivot)
-            roots = jnp.where(line == i, root, roots)
-            if i < 7:
-                beside = spread(cols[i][0][i + 1 : i + 2, :]) * root
-                pivot = spread(cols[i + 1][0][i + 1 : i + 2, :]) - beside * beside
-            by = [c * root for c in cols[i]]
-            for j in range(i + 1, 8):
-                row = spread(cols[j][0][i : i + 1, :]) * root
-                cols[j] = [c - b * row for c, b in zip(cols[j], by)]
-            by[0] = jnp.where(line > i, by[0], 0.0)
-            row = spread(a[t][i : i + 1, :]) * root
+            roots = root if k == 0 else jnp.where(line == k, root, roots)
+            if i + 1 < WIDTH:
+                p, q = divmod(i + 1, 8)
+                beside = spread(cols[i][p][q : q + 1, :]) * root
+                pivot = spread(cols[i + 1][p][q : q + 1, :]) - beside * beside
+            by = [c * root for c in cols[i][at:]]
+            for j in range(i + 1, WIDTH):
+                row = spread(cols[j][at][k : k + 1, :]) * root
+                cols[j] = cols[j][:at] + [c - b * row for c, b in zip(cols[j][at:], by)]
+            row = spread(a[top + at][k : k + 1, :]) * root
+            by[0] = jnp.where(line > k, by[0], 0.0)
             for r, b in enumerate(by):
-                a[t + r] = a[t + r] - b * row
-        a[t] = a[t] * roots
+                a[top + at + r] = a[top + at + r] - b * row
+            if k == 7:
+                a[top + at] = a[top + at] * roots
     return jnp.concatenate([piece[:, :n] for piece in a], axis=0)
 
 
@@ -315,11 +327,10 @@
 
 
 def sum_everywhere(x):
-    near = ("x", "core")
+    near, far = ("z_low", "x", "core"), ("z_high", "y")
     parts = x.reshape(lax.axis_size(near), -1, x.shape[1])
     own = summed(exchange(parts, near))
-    own = summed(from_everyone(own, "y"))
-    own = summed(from_everyone(own, "grp"))
+    own = summed(from_everyone(own, far))
     return from_everyone(own, near).reshape(x.shape)
 
 
@@ -330,7 +341,7 @@
 
 
 def solution(mesh):
-    torus = Mesh(mesh.devices.reshape(mesh.shape["grp"], 8, 4, 2), AXES)
+    torus = Mesh(mesh.devices.reshape(mesh.shape["grp"] // 2, 2, 8, 4, 2), AXES)
     return jax.shard_map(
         on_device,
         mesh=torus,

time: 101 us -> 97.1 us (0.961)
  local copies, waits for them, and re-layouts: 2.98 us -> 0.04 us
  blocking collectives: 46.9 us -> 44.3 us
  waiting for transfers between devices: 12 us -> 13.6 us
    unnamed x4 -> x0, local copies, waits for them, and re-layouts: 2.93 us -> none
    all_to_all x4 -> x3, blocking collectives: 46.9 us -> 44.3 us  [exchange(): return lax.all_to_all(x, axes, split_axis=0, concat_axis=0, tiled=True)]
    ppermute x4, waiting for transfers between devices: 12 us -> 13.6 us  [exchanged(): return lax.ppermute(x, AXES, pairs).reshape(shape)]
  transfers between devices with their start and end apart: 4 -> 4, of which waited for: 2 -> 2; matrix products, arithmetic and copies ran while one was open for 1% -> 1% of each run, Pallas kernels for 1% -> 3%
where the time goes in v3:
time: 97.1 us; the launch traced here: 96.8 us
  blocking collectives  44.3 us (46%)
  starting transfers between devices  23 us (24%)
  Pallas kernels  14.3 us (15%)
  waiting for transfers between devices  13.6 us (14%)
    all_to_all x3, blocking collectives, exchange(): return lax.all_to_all(x, axes, split_axis=0, concat_axis=0, tiled=True)  44.3 us
    ppermute x4, starting transfers between devices, exchanged(): return lax.ppermute(x, AXES, pairs).reshape(shape)  23 us
    ppermute x4, waiting for transfers between devices, exchanged(): return lax.ppermute(x, AXES, pairs).reshape(shape)  13.6 us
    pallas_call x1, Pallas kernels, next_basis(): pl.pallas_call(functools.partial(next_kernel, rows_total), out_shape=jax....  8.19 us
    pallas_call x3, Pallas kernels, kernel_call(): pl.pallas_call(body, out_shape=tuple(outs), in_specs=ins, out_specs=(VMEM...  5.69 us
  transfers between devices with their start and end apart: 4, of which 2 were waited for; matrix products, arithmetic and copies ran while one was open for 1% of the time, Pallas kernels for 3%

profile of v3, /device:TPU:1, one launch (start us, length us, event | category | flops | bytes accessed | tf_op | source)
XLA Modules:
  0.0 96.8 jit_solution(11140673801710610694)
XLA Ops:
  0.0 8.7 %collective-permute-start = (bf16[1024,256]{1,0:T(8,128)(2,1)}, bf16[1024,256]{1,0:T(8,128)(2,1)S(1)}, u32[]{:S(2)}, u32[]{:S(2)}) collective-permute-start(bf16[1024,256]{1,0:T(8,128)(2,1)} %param.9), channel_id=1, source_target_pairs={{0,1},{1,0},{2,3},{3,2},{4,5},{5,4},{6,7},{7,6},{8,9},{9,8},{10,11... | collective-permute-start | bytes 1572872 | tf_op jit(solution)/shard_map/ppermute | solution.py:147
  8.7 1.9 %collective-permute-start.1 = (bf16[1024,256]{1,0:T(8,128)(2,1)}, bf16[1024,256]{1,0:T(8,128)(2,1)S(1)}, u32[]{:S(2)}, u32[]{:S(2)}) collective-permute-start(bf16[1024,256]{1,0:T(8,128)(2,1)} %param.9), channel_id=1, source_target_pairs={{0,511},{1,2},{2,1},{3,4},{4,3},{5,6},{6,5},{7,8},{8,7},{9,10},{10... | collective-permute-start | bytes 1572872 | tf_op jit(solution)/shard_map/ppermute | solution.py:147
  11.3 0.7 pad_add_fusion.table
  12.1 0.0 collective-permute-done
  12.1 2.6 %shard_map.55 = (bf16[6,512,512]{2,1,0:T(8,128)(2,1)S(1)}, f32[2,512,256]{2,1,0:T(8,128)S(1)}) custom-call(s32[13]{0:T(128)S(1)} %pad_add_fusion.table, bf16[6,512,512]{2,1,0:T(8,128)(2,1)} %tiles_ref.1, bf16[2,512,256]{2,1,0:T(8,128)(2,1)} %bitcast.15, bf16[2,512,256]{2,1,0:T(8,128)(2,1)S(1)} %bitcast.10), custom_call_target="tpu_custom_call" | custom-call | flops 805306368 | bytes 4194304 | tf_op jit(solution)/shard_map/pallas_call | solution.py:131
  14.7 4.8 %collective-permute-done.1 = bf16[1024,256]{1,0:T(8,128)(2,1)S(1)} collective-permute-done((bf16[1024,256]{1,0:T(8,128)(2,1)}, bf16[1024,256]{1,0:T(8,128)(2,1)S(1)}, u32[]{:S(2)}, u32[]{:S(2)}) %collective-permute-start.1) | collective-permute-done | bytes 524320 | tf_op jit(solution)/shard_map/ppermute | solution.py:147
  19.5 1.6 %shard_map.56 = (bf16[2,512,256]{2,1,0:T(8,128)(2,1)S(1)}, bf16[2,512,256]{2,1,0:T(8,128)(2,1)S(1)}) custom-call(s32[13]{0:T(128)S(1)} %pad_add_fusion.table, bf16[6,512,512]{2,1,0:T(8,128)(2,1)S(1)} %get-tuple-element.13.held_ref, f32[2,512,256]{2,1,0:T(8,128)S(1)} %get-tuple-element.14.acc_in, bf16[2,512,256]{2,1,0:T(8,128)(2,1)S(1)} %bitcast.9), custom_call_target="tpu_custom_call" | custom-call | flops 805306368 | bytes 4194304 | tf_op jit(solution)/shard_map/pallas_call | solution.py:131
  21.1 1.5 %shard_map.57 = (bf16[2,512,256]{2,1,0:T(8,128)(2,1)S(1)}, f32[2,512,256]{2,1,0:T(8,128)S(1)}) custom-call(s32[13]{0:T(128)S(1)} %pad_add_fusion.table, bf16[6,512,512]{2,1,0:T(8,128)(2,1)S(1)} %get-tuple-element.13.held_ref, bf16[2,512,256]{2,1,0:T(8,128)(2,1)S(1)} %get-tuple-element.15.aq_ref), custom_call_target="tpu_custom_call" | custom-call | flops 805306368 | bytes 4194304 | tf_op jit(solution)/shard_map/pallas_call | solution.py:131
  22.6 10.4 %collective-permute-start.3 = (bf16[2,512,256]{2,1,0:T(8,128)(2,1)S(1)}, bf16[2,512,256]{2,1,0:T(8,128)(2,1)S(1)}, u32[]{:S(2)}, u32[]{:S(2)}) collective-permute-start(bf16[2,512,256]{2,1,0:T(8,128)(2,1)S(1)} %get-tuple-element.18), channel_id=1, source_target_pairs={{0,1},{1,0},{2,3},{3,2},{4,5},{5,4},{6,7},{7,6},{8,9},{9,8},{10,11... | collective-permute-start | bytes 1572872 | tf_op jit(solution)/shard_map/ppermute | solution.py:147
  33.0 1.9 %collective-permute-start.2 = (bf16[2,512,256]{2,1,0:T(8,128)(2,1)S(1)}, bf16[2,512,256]{2,1,0:T(8,128)(2,1)S(1)}, u32[]{:S(2)}, u32[]{:S(2)}) collective-permute-start(bf16[2,512,256]{2,1,0:T(8,128)(2,1)S(1)} %get-tuple-element.17), channel_id=1, source_target_pairs={{0,511},{1,2},{2,1},{3,4},{4,3},{5,6},{6,5},{7,8},{8,7},{9,10},{10... | collective-permute-start | bytes 1572872 | tf_op jit(solution)/shard_map/ppermute | solution.py:147
  35.0 0.0 collective-permute-done.3
  35.0 8.9 %collective-permute-done.2 = bf16[2,512,256]{2,1,0:T(8,128)(2,1)S(1)} collective-permute-done((bf16[2,512,256]{2,1,0:T(8,128)(2,1)S(1)}, bf16[2,512,256]{2,1,0:T(8,128)(2,1)S(1)}, u32[]{:S(2)}, u32[]{:S(2)}) %collective-permute-start.2) | collective-permute-done | bytes 524320 | tf_op jit(solution)/shard_map/ppermute | solution.py:147
  43.8 0.4 gram.1
  44.2 13.5 %all_to_all.15 = bf16[16,24,128]{2,1,0:T(8,128)(2,1)S(1)} all-to-all(bf16[16,24,128]{2,1,0:T(8,128)(2,1)S(1)} %bitcast.14), channel_id=1, replica_groups=mesh['z_high'=4,'z_low'=2,'y'=8,'x'=4,'core'=2] {'z_low','x','core'}, dimensions={0} | all-to-all | bytes 196608 | tf_op jit(solution)/shard_map/all_to_all | solution.py:322
  57.7 19.6 %all_to_all.16 = bf16[32,24,128]{2,1,0:T(8,128)(2,1)S(1)} all-to-all(bf16[32,24,128]{2,1,0:T(8,128)(2,1)S(1)} %broadcast_in_dim.6), channel_id=1, replica_groups=mesh['z_high'=4,'z_low'=2,'y'=8,'x'=4,'core'=2] {'z_high','y'}, dimensions={0} | all-to-all | bytes 393216 | tf_op jit(solution)/shard_map/all_to_all | solution.py:322
  77.4 11.2 %all_to_all.17 = bf16[16,24,128]{2,1,0:T(8,128)(2,1)S(1)} all-to-all(bf16[16,24,128]{2,1,0:T(8,128)(2,1)S(1)} %broadcast_in_dim.7), channel_id=1, replica_groups=mesh['z_high'=4,'z_low'=2,'y'=8,'x'=4,'core'=2] {'z_low','x','core'}, dimensions={0} | all-to-all | bytes 196608 | tf_op jit(solution)/shard_map/all_to_all | solution.py:322
  88.6 8.2 %next_basis.1 = f32[1024,256]{1,0:T(8,128)} custom-call(bf16[384,128]{1,0:T(8,128)(2,1)S(1)} %bitcast.13, f32[1024,256]{1,0:T(8,128)S(1)} %get-tuple-element.20.y_ref), custom_call_target="tpu_custom_call" | custom-call | flops 402653184 | bytes 2097152 | tf_op jit(solution)/shard_map/next_basis/pallas_call | solution.py:304
  (4 shorter events, 0.1 us)
Async XLA Ops:
  0.0 12.1 %collective-permute-start = (bf16[1024,256]{1,0:T(8,128)(2,1)}, bf16[1024,256]{1,0:T(8,128)(2,1)S(1)}, u32[]{:S(2)}, u32[]{:S(2)}) collective-permute-start(bf16[1024,256]{1,0:T(8,128)(2,1)} %param.9), channel_id=1, source_target_pairs={{0,1},{1,0},{2,3},{3,2},{4,5},{5,4},{6,7},{7,6},{8,9},{9,8},{10,11... | collective-permute-start | bytes 1572872 | tf_op jit(solution)/shard_map/ppermute | solution.py:147
  8.7 10.7 %collective-permute-start.1 = (bf16[1024,256]{1,0:T(8,128)(2,1)}, bf16[1024,256]{1,0:T(8,128)(2,1)S(1)}, u32[]{:S(2)}, u32[]{:S(2)}) collective-permute-start(bf16[1024,256]{1,0:T(8,128)(2,1)} %param.9), channel_id=1, source_target_pairs={{0,511},{1,2},{2,1},{3,4},{4,3},{5,6},{6,5},{7,8},{8,7},{9,10},{10... | collective-permute-start | bytes 1572872 | tf_op jit(solution)/shard_map/ppermute | solution.py:147
  22.6 12.4 %collective-permute-start.3 = (bf16[2,512,256]{2,1,0:T(8,128)(2,1)S(1)}, bf16[2,512,256]{2,1,0:T(8,128)(2,1)S(1)}, u32[]{:S(2)}, u32[]{:S(2)}) collective-permute-start(bf16[2,512,256]{2,1,0:T(8,128)(2,1)S(1)} %get-tuple-element.18), channel_id=1, source_target_pairs={{0,1},{1,0},{2,3},{3,2},{4,5},{5,4},{6,7},{7,6},{8,9},{9,8},{10,11... | collective-permute-start | bytes 1572872 | tf_op jit(solution)/shard_map/ppermute | solution.py:147
  33.0 10.8 %collective-permute-start.2 = (bf16[2,512,256]{2,1,0:T(8,128)(2,1)S(1)}, bf16[2,512,256]{2,1,0:T(8,128)(2,1)S(1)}, u32[]{:S(2)}, u32[]{:S(2)}) collective-permute-start(bf16[2,512,256]{2,1,0:T(8,128)(2,1)S(1)} %get-tuple-element.17), channel_id=1, source_target_pairs={{0,511},{1,2},{2,1},{3,4},{4,3},{5,6},{6,5},{7,8},{8,7},{9,10},{10... | collective-permute-start | bytes 1572872 | tf_op jit(solution)/shard_map/ppermute | solution.py:147

commit v4 on v3

--- a/solution.py
+++ b/solution.py
@@ -18,6 +18,11 @@
 
 def dot(a, b, ca, cb):
     return lax.dot_general(a, b, (((ca,), (cb,)), ((), ())), preferred_element_type=F32)
+
+
+def split(x):
+    hi = x.astype(BF16)
+    return hi, (x - hi.astype(F32)).astype(BF16)
 
 
 SMEM = pl.BlockSpec(memory_space=pltpu.SMEM)
@@ -183,53 +188,60 @@
     return sums.reshape(rows, k), from_across, from_beside
 
 
-def gram_kernel(own_ref, below_ref, above_ref, y_ref, gram_ref):
-    y = own_ref[...] + below_ref[...].astype(F32) + above_ref[...].astype(F32)
-    y_ref[...] = y
+def gram_kernel(own_ref, across_ref, beside_ref, hi_ref, lo_ref, y_ref, gram_ref):
+    half = y_ref.shape[1]
+    y = own_ref[...] + across_ref[...].astype(F32) + beside_ref[...].astype(F32)
+    hi, lo = split(y[:, :half])
+    hi_ref[...] = hi
+    lo_ref[...] = lo
+    y_ref[...] = y[:, half:]
     b = y.astype(BF16)
-    half = b.shape[1] // 2
     full = dot(b, b, 0, 0)
     gram_ref[0:half, :] = full[:half, :half].astype(BF16)
-    gram_ref[half : 2 * half, :] = full[:half, half:].astype(BF16)
+    gram_ref[half : 2 * half, :] = full[half:, :half].astype(BF16)
     gram_ref[2 * half :, :] = full[half:, half:].astype(BF16)
 
 
-def gram(own, below, above):
+def gram(own, across, beside):
     rows, k = own.shape
-    vmem = pl.BlockSpec(memory_space=pltpu.VMEM)
     return pl.pallas_call(
         gram_kernel,
         out_shape=(
-            jax.ShapeDtypeStruct((rows, k), F32),
+            jax.ShapeDtypeStruct((rows, k // 2), BF16),
+            jax.ShapeDtypeStruct((rows, k // 2), BF16),
+            jax.ShapeDtypeStruct((rows, k // 2), F32),
             jax.ShapeDtypeStruct((3 * k // 2, k // 2), BF16),
         ),
-        in_specs=[vmem] * 3,
-        out_specs=(vmem,) * 2,
+        in_specs=[VMEM] * 3,
+        out_specs=(VMEM,) * 4,
         compiler_params=pltpu.CompilerParams(vmem_limit_bytes=32 << 20),
         cost_estimate=pl.CostEstimate(
             flops=2 * rows * k * k, bytes_accessed=8 * rows * k, transcendentals=0
         ),
         name="gram",
-    )(own, below, above)
+    )(own, across, beside)
 
 
 def spread(piece):
     return jnp.broadcast_to(piece, (8, 128))
 
 
-def leaf_inverse(d, zero):
+def leaf_inverse(d, zero, left=None):
     n = d.shape[0]
     pieces = n // 8
     eye = (
         lax.broadcasted_iota(jnp.int32, (n, n), 0) == lax.broadcasted_iota(jnp.int32, (n, n), 1)
     ).astype(F32)
-    both = jnp.concatenate([eye, d], axis=1)
-    a = [both[8 * r : 8 * r + 8, :] for r in range(pieces)]
+    wide = [jnp.concatenate([eye, d], axis=1)]
+    if left is not None:
+        wide.append(jnp.concatenate([left, left], axis=1))
+    a = [[part[8 * r : 8 * r + 8, :] for part in wide] for r in range(pieces)]
     line = lax.broadcasted_iota(jnp.int32, (8, 128), 0)
     for first in range(0, n, WIDTH):
         top = first // 8
+
         cols = [
-            [spread(a[r][:, n + first + i : n + first + i + 1]) for r in range(top, pieces)]
+            [spread(a[r][0][:, n + first + i : n + first + i + 1]) for r in range(top, pieces)]
             for i in range(WIDTH)
         ]
         for col in cols:
@@ -248,70 +260,84 @@
             for j in range(i + 1, WIDTH):
                 row = spread(cols[j][at][k : k + 1, :]) * root
                 cols[j] = cols[j][:at] + [c - b * row for c, b in zip(cols[j][at:], by)]
-            row = spread(a[top + at][k : k + 1, :]) * root
+            rows = [spread(part[k : k + 1, :]) * root for part in a[top + at]]
             by[0] = jnp.where(line > k, by[0], 0.0)
             for r, b in enumerate(by):
-                a[top + at + r] = a[top + at + r] - b * row
+                a[top + at + r] = [p - b * row for p, row in zip(a[top + at + r], rows)]
             if k == 7:
-                a[top + at] = a[top + at] * roots
-    return jnp.concatenate([piece[:, :n] for piece in a], axis=0)
-
-
-def split(x):
-    hi = x.astype(BF16)
-    return hi, (x - hi.astype(F32)).astype(BF16)
+                a[top + at] = [part * roots for part in a[top + at]]
+    done = [jnp.concatenate([piece[i][:, :n] for piece in a], axis=0) for i in range(len(wide))]
+    return done[0] if left is None else tuple(done)
 
 
 def dot3(a, b, ca, cb):
-    a_hi, a_lo = split(a)
-    b_hi, b_lo = split(b)
+    (a_hi, a_lo), (b_hi, b_lo) = a, b
     return dot(a_hi, b_hi, ca, cb) + (dot(a_lo, b_hi, ca, cb) + dot(a_hi, b_lo, ca, cb))
 
 
-def factor_inverse(g, zero):
-    g11, g12, g22 = g
-    x11 = whole_inverse(g11, zero)
-    b = dot3(x11, g12, 1, 0)
-    s = g22 - dot3(b, b, 0, 0)
-    x22 = whole_inverse(s, zero)
-    x21 = -dot3(x22, dot3(b, x11, 0, 0), 1, 0)
-    return x11, x21, x22
-
-
-def joined(x11, x21, x22):
+def eliminated(x11, d21, d22):
+    x11 = split(x11)
+    l21 = split(dot3(split(d21), x11, 1, 1))
+    return x11, l21, d22 - dot3(l21, l21, 1, 1)
+
+
+def factor_inverse(d, zero):
+    h = LEAF
+    x11 = leaf_inverse(d[:h, :h], zero)
+    s11, l21, s = eliminated(x11, d[h:, :h], d[h:, h:])
+    x22, x21 = leaf_inverse(s, zero, -dot3(l21, s11, 1, 0))
     upper = jnp.concatenate([x11, jnp.zeros_like(x11)], axis=1)
     return jnp.concatenate([upper, jnp.concatenate([x21, x22], axis=1)], axis=0)
 
 
-def whole_inverse(d, zero):
-    n = d.shape[0]
-    if n == LEAF:
-        return leaf_inverse(d, zero)
-    h = n // 2
-    return joined(*factor_inverse((d[:h, :h], d[:h, h:], d[h:, h:]), zero))
-
-
-def next_kernel(rows_total, gram_ref, y_ref, out_ref):
+CHUNKS = 4
+
+
+def next_kernel(rows_total, gram_ref, hi_ref, lo_ref, y_ref, out_ref, first, second, rest, sems):
     half = gram_ref.shape[1]
-    g = [gram_ref[pl.ds(i * half, half), :].astype(F32) / rows_total for i in range(3)]
-    x = joined(*factor_inverse(g, y_ref[0:8, 0:128] * 0.0))
-    out_ref[...] = dot3(y_ref[...], x, 1, 1)
-
-
-def next_basis(rows_total, packed, y):
-    rows, k = y.shape
-    vmem = pl.BlockSpec(memory_space=pltpu.VMEM)
+    step = y_ref.shape[0] // CHUNKS
+    d11, d21, d22 = (
+        gram_ref[pl.ds(i * half, half), :].astype(F32) / rows_total for i in range(3)
+    )
+    zero = y_ref[0:8, 0:128] * 0.0
+    x11, l21, s = eliminated(factor_inverse(d11, zero), d21, d22)
+    q1 = dot3((hi_ref[...], lo_ref[...]), x11, 1, 1)
+    first[...] = q1
+    copies = [pltpu.make_async_copy(first, out_ref.at[:, pl.ds(0, half)], sems.at[CHUNKS])]
+    copies[0].start()
+    rest[0], rest[1] = split(y_ref[...] - dot3(split(q1), l21, 1, 1))
+    x22 = split(factor_inverse(s, zero))
+    for i in range(CHUNKS):
+        rows = pl.ds(i * step, step)
+        second[rows, :] = dot3((rest[0, rows, :], rest[1, rows, :]), x22, 1, 1)
+        copy = pltpu.make_async_copy(
+            second.at[rows], out_ref.at[rows, pl.ds(half, half)], sems.at[i]
+        )
+        copy.start()
+        copies.append(copy)
+    for copy in copies:
+        copy.wait()
+
+
+def next_basis(rows_total, packed, hi, lo, y):
+    rows, half = y.shape
     return pl.pallas_call(
         functools.partial(next_kernel, rows_total),
-        out_shape=jax.ShapeDtypeStruct((rows, k), F32),
-        in_specs=[vmem] * 2,
-        out_specs=vmem,
+        out_shape=jax.ShapeDtypeStruct((rows, 2 * half), F32),
+        in_specs=[VMEM] * 4,
+        out_specs=HBM,
+        scratch_shapes=[
+            pltpu.VMEM((rows, half), F32),
+            pltpu.VMEM((rows, half), F32),
+            pltpu.VMEM((2, rows, half), BF16),
+            pltpu.SemaphoreType.DMA((CHUNKS + 1,)),
+        ],
         compiler_params=pltpu.CompilerParams(vmem_limit_bytes=32 << 20),
         cost_estimate=pl.CostEstimate(
-            flops=6 * rows * k * k, bytes_accessed=8 * rows * k, transcendentals=0
+            flops=24 * rows * half * half, bytes_accessed=16 * rows * half, transcendentals=0
         ),
         name="next_basis",
-    )(packed, y)
+    )(packed, hi, lo, y)
 
 
 def summed(x):
@@ -336,8 +362,8 @@
 
 def on_device(tiles, tile_row, tile_col, tile_count, q_block):
     rows_total = q_block.shape[0] * lax.axis_size(AXES)
-    y, packed = gram(*band(tiles, tile_row, tile_col, tile_count, q_block))
-    return next_basis(rows_total, sum_everywhere(packed), y)
+    hi, lo, y, packed = gram(*band(tiles, tile_row, tile_col, tile_count, q_block))
+    return next_basis(rows_total, sum_everywhere(packed), hi, lo, y)
 
 
 def solution(mesh):

time: 97.1 us -> 96.9 us (level)
  no operation moved by 1% of the time
where the time goes in v4:
time: 96.9 us; the launch traced here: 96.6 us
  blocking collectives  44.3 us (46%)
  starting transfers between devices  23 us (24%)
  Pallas kernels  13.9 us (14%)
  waiting for transfers between devices  13.6 us (14%)
    all_to_all x3, blocking collectives, exchange(): return lax.all_to_all(x, axes, split_axis=0, concat_axis=0, tiled=True)  44.3 us
    ppermute x4, starting transfers between devices, exchanged(): return lax.ppermute(x, AXES, pairs).reshape(shape)  23 us
    ppermute x4, waiting for transfers between devices, exchanged(): return lax.ppermute(x, AXES, pairs).reshape(shape)  13.6 us
    pallas_call x1, Pallas kernels, next_basis(): pl.pallas_call(functools.partial(next_kernel, rows_total), out_shape=jax....  7.8 us
    pallas_call x3, Pallas kernels, kernel_call(): pl.pallas_call(body, out_shape=tuple(outs), in_specs=ins, out_specs=(VMEM...  5.69 us
  transfers between devices with their start and end apart: 4, of which 2 were waited for; matrix products, arithmetic and copies ran while one was open for 1% of the time, Pallas kernels for 3%

profile of v4, /device:TPU:1, one launch (start us, length us, event | category | flops | bytes accessed | tf_op | source)
XLA Modules:
  0.0 96.6 jit_solution(17324315234226454425)
XLA Ops:
  0.0 8.7 %collective-permute-start = (bf16[1024,256]{1,0:T(8,128)(2,1)}, bf16[1024,256]{1,0:T(8,128)(2,1)S(1)}, u32[]{:S(2)}, u32[]{:S(2)}) collective-permute-start(bf16[1024,256]{1,0:T(8,128)(2,1)} %param.9), channel_id=1, source_target_pairs={{0,1},{1,0},{2,3},{3,2},{4,5},{5,4},{6,7},{7,6},{8,9},{9,8},{10,11... | collective-permute-start | bytes 1572872 | tf_op jit(solution)/shard_map/ppermute | solution.py:152
  8.7 1.9 %collective-permute-start.1 = (bf16[1024,256]{1,0:T(8,128)(2,1)}, bf16[1024,256]{1,0:T(8,128)(2,1)S(1)}, u32[]{:S(2)}, u32[]{:S(2)}) collective-permute-start(bf16[1024,256]{1,0:T(8,128)(2,1)} %param.9), channel_id=1, source_target_pairs={{0,511},{1,2},{2,1},{3,4},{4,3},{5,6},{6,5},{7,8},{8,7},{9,10},{10... | collective-permute-start | bytes 1572872 | tf_op jit(solution)/shard_map/ppermute | solution.py:152
  11.3 0.7 pad_add_fusion.table
  12.1 0.0 collective-permute-done
  12.1 2.6 %shard_map.55 = (bf16[6,512,512]{2,1,0:T(8,128)(2,1)S(1)}, f32[2,512,256]{2,1,0:T(8,128)S(1)}) custom-call(s32[13]{0:T(128)S(1)} %pad_add_fusion.table, bf16[6,512,512]{2,1,0:T(8,128)(2,1)} %tiles_ref.1, bf16[2,512,256]{2,1,0:T(8,128)(2,1)} %bitcast.15, bf16[2,512,256]{2,1,0:T(8,128)(2,1)S(1)} %bitcast.10), custom_call_target="tpu_custom_call" | custom-call | flops 805306368 | bytes 4194304 | tf_op jit(solution)/shard_map/pallas_call | solution.py:136
  14.7 4.8 %collective-permute-done.1 = bf16[1024,256]{1,0:T(8,128)(2,1)S(1)} collective-permute-done((bf16[1024,256]{1,0:T(8,128)(2,1)}, bf16[1024,256]{1,0:T(8,128)(2,1)S(1)}, u32[]{:S(2)}, u32[]{:S(2)}) %collective-permute-start.1) | collective-permute-done | bytes 524320 | tf_op jit(solution)/shard_map/ppermute | solution.py:152
  19.5 1.6 %shard_map.56 = (bf16[2,512,256]{2,1,0:T(8,128)(2,1)S(1)}, bf16[2,512,256]{2,1,0:T(8,128)(2,1)S(1)}) custom-call(s32[13]{0:T(128)S(1)} %pad_add_fusion.table, bf16[6,512,512]{2,1,0:T(8,128)(2,1)S(1)} %get-tuple-element.15.held_ref, f32[2,512,256]{2,1,0:T(8,128)S(1)} %get-tuple-element.16.acc_in, bf16[2,512,256]{2,1,0:T(8,128)(2,1)S(1)} %bitcast.9), custom_call_target="tpu_custom_call" | custom-call | flops 805306368 | bytes 4194304 | tf_op jit(solution)/shard_map/pallas_call | solution.py:136
  21.1 1.5 %shard_map.57 = (bf16[2,512,256]{2,1,0:T(8,128)(2,1)S(1)}, f32[2,512,256]{2,1,0:T(8,128)S(1)}) custom-call(s32[13]{0:T(128)S(1)} %pad_add_fusion.table, bf16[6,512,512]{2,1,0:T(8,128)(2,1)S(1)} %get-tuple-element.15.held_ref, bf16[2,512,256]{2,1,0:T(8,128)(2,1)S(1)} %get-tuple-element.17.aq_ref), custom_call_target="tpu_custom_call" | custom-call | flops 805306368 | bytes 4194304 | tf_op jit(solution)/shard_map/pallas_call | solution.py:136
  22.6 10.4 %collective-permute-start.3 = (bf16[2,512,256]{2,1,0:T(8,128)(2,1)S(1)}, bf16[2,512,256]{2,1,0:T(8,128)(2,1)S(1)}, u32[]{:S(2)}, u32[]{:S(2)}) collective-permute-start(bf16[2,512,256]{2,1,0:T(8,128)(2,1)S(1)} %get-tuple-element.20), channel_id=1, source_target_pairs={{0,1},{1,0},{2,3},{3,2},{4,5},{5,4},{6,7},{7,6},{8,9},{9,8},{10,11... | collective-permute-start | bytes 1572872 | tf_op jit(solution)/shard_map/ppermute | solution.py:152
  33.0 1.9 %collective-permute-start.2 = (bf16[2,512,256]{2,1,0:T(8,128)(2,1)S(1)}, bf16[2,512,256]{2,1,0:T(8,128)(2,1)S(1)}, u32[]{:S(2)}, u32[]{:S(2)}) collective-permute-start(bf16[2,512,256]{2,1,0:T(8,128)(2,1)S(1)} %get-tuple-element.19), channel_id=1, source_target_pairs={{0,511},{1,2},{2,1},{3,4},{4,3},{5,6},{6,5},{7,8},{8,7},{9,10},{10... | collective-permute-start | bytes 1572872 | tf_op jit(solution)/shard_map/ppermute | solution.py:152
  35.0 0.0 collective-permute-done.3
  35.0 8.9 %collective-permute-done.2 = bf16[2,512,256]{2,1,0:T(8,128)(2,1)S(1)} collective-permute-done((bf16[2,512,256]{2,1,0:T(8,128)(2,1)S(1)}, bf16[2,512,256]{2,1,0:T(8,128)(2,1)S(1)}, u32[]{:S(2)}, u32[]{:S(2)}) %collective-permute-start.2) | collective-permute-done | bytes 524320 | tf_op jit(solution)/shard_map/ppermute | solution.py:152
  43.8 0.4 gram.1
  44.3 13.5 %all_to_all.15 = bf16[16,24,128]{2,1,0:T(8,128)(2,1)S(1)} all-to-all(bf16[16,24,128]{2,1,0:T(8,128)(2,1)S(1)} %bitcast.14), channel_id=1, replica_groups=mesh['z_high'=4,'z_low'=2,'y'=8,'x'=4,'core'=2] {'z_low','x','core'}, dimensions={0} | all-to-all | bytes 196608 | tf_op jit(solution)/shard_map/all_to_all | solution.py:348
  57.8 19.6 %all_to_all.16 = bf16[32,24,128]{2,1,0:T(8,128)(2,1)S(1)} all-to-all(bf16[32,24,128]{2,1,0:T(8,128)(2,1)S(1)} %broadcast_in_dim.6), channel_id=1, replica_groups=mesh['z_high'=4,'z_low'=2,'y'=8,'x'=4,'core'=2] {'z_high','y'}, dimensions={0} | all-to-all | bytes 393216 | tf_op jit(solution)/shard_map/all_to_all | solution.py:348
  77.4 11.2 %all_to_all.17 = bf16[16,24,128]{2,1,0:T(8,128)(2,1)S(1)} all-to-all(bf16[16,24,128]{2,1,0:T(8,128)(2,1)S(1)} %broadcast_in_dim.7), channel_id=1, replica_groups=mesh['z_high'=4,'z_low'=2,'y'=8,'x'=4,'core'=2] {'z_low','x','core'}, dimensions={0} | all-to-all | bytes 196608 | tf_op jit(solution)/shard_map/all_to_all | solution.py:348
  88.7 7.8 %next_basis.1 = f32[1024,256]{1,0:T(8,128)} custom-call(bf16[384,128]{1,0:T(8,128)(2,1)S(1)} %bitcast.13, bf16[1024,128]{1,0:T(8,128)(2,1)S(1)} %get-tuple-element.22.hi_ref, bf16[1024,128]{1,0:T(8,128)(2,1)S(1)} %get-tuple-element.23.lo_ref, f32[1024,128]{1,0:T(8,128)S(1)} %get-tuple-element.24.y_ref), custom_call_target="tpu_custom_call" | custom-call | flops 402653184 | bytes 2097152 | tf_op jit(solution)/shard_map/next_basis/pallas_call | solution.py:324
  (4 shorter events, 0.1 us)
Async XLA Ops:
  0.0 12.1 %collective-permute-start = (bf16[1024,256]{1,0:T(8,128)(2,1)}, bf16[1024,256]{1,0:T(8,128)(2,1)S(1)}, u32[]{:S(2)}, u32[]{:S(2)}) collective-permute-start(bf16[1024,256]{1,0:T(8,128)(2,1)} %param.9), channel_id=1, source_target_pairs={{0,1},{1,0},{2,3},{3,2},{4,5},{5,4},{6,7},{7,6},{8,9},{9,8},{10,11... | collective-permute-start | bytes 1572872 | tf_op jit(solution)/shard_map/ppermute | solution.py:152
  8.7 10.7 %collective-permute-start.1 = (bf16[1024,256]{1,0:T(8,128)(2,1)}, bf16[1024,256]{1,0:T(8,128)(2,1)S(1)}, u32[]{:S(2)}, u32[]{:S(2)}) collective-permute-start(bf16[1024,256]{1,0:T(8,128)(2,1)} %param.9), channel_id=1, source_target_pairs={{0,511},{1,2},{2,1},{3,4},{4,3},{5,6},{6,5},{7,8},{8,7},{9,10},{10... | collective-permute-start | bytes 1572872 | tf_op jit(solution)/shard_map/ppermute | solution.py:152
  22.6 12.4 %collective-permute-start.3 = (bf16[2,512,256]{2,1,0:T(8,128)(2,1)S(1)}, bf16[2,512,256]{2,1,0:T(8,128)(2,1)S(1)}, u32[]{:S(2)}, u32[]{:S(2)}) collective-permute-start(bf16[2,512,256]{2,1,0:T(8,128)(2,1)S(1)} %get-tuple-element.20), channel_id=1, source_target_pairs={{0,1},{1,0},{2,3},{3,2},{4,5},{5,4},{6,7},{7,6},{8,9},{9,8},{10,11... | collective-permute-start | bytes 1572872 | tf_op jit(solution)/shard_map/ppermute | solution.py:152
  33.0 10.8 %collective-permute-start.2 = (bf16[2,512,256]{2,1,0:T(8,128)(2,1)S(1)}, bf16[2,512,256]{2,1,0:T(8,128)(2,1)S(1)}, u32[]{:S(2)}, u32[]{:S(2)}) collective-permute-start(bf16[2,512,256]{2,1,0:T(8,128)(2,1)S(1)} %get-tuple-element.19), channel_id=1, source_target_pairs={{0,511},{1,2},{2,1},{3,4},{4,3},{5,6},{6,5},{7,8},{8,7},{9,10},{10... | collective-permute-start | bytes 1572872 | tf_op jit(solution)/shard_map/ppermute | solution.py:152

commit v5 on v4

--- a/solution.py
+++ b/solution.py
@@ -11,7 +11,7 @@
 H = 2
 LEAF = 64
 WIDTH = 16
-AXES = ("z_high", "z_low", "y", "x", "core")
+AXES = ("z", "y_high", "y_low", "x", "core")
 F32 = jnp.float32
 BF16 = jnp.bfloat16
 
@@ -353,7 +353,7 @@
 
 
 def sum_everywhere(x):
-    near, far = ("z_low", "x", "core"), ("z_high", "y")
+    near, far = ("y_low", "x", "core"), ("z", "y_high")
     parts = x.reshape(lax.axis_size(near), -1, x.shape[1])
     own = summed(exchange(parts, near))
     own = summed(from_everyone(own, far))
@@ -367,7 +367,7 @@
 
 
 def solution(mesh):
-    torus = Mesh(mesh.devices.reshape(mesh.shape["grp"] // 2, 2, 8, 4, 2), AXES)
+    torus = Mesh(mesh.devices.reshape(mesh.shape["grp"], 4, 2, 4, 2), AXES)
     return jax.shard_map(
         on_device,
         mesh=torus,

time: 96.9 us -> 96.1 us (level)
  no operation moved by 1% of the time
where the time goes in v5:
time: 96.1 us; the launch traced here: 95.7 us
  blocking collectives  43.4 us (45%)
  starting transfers between devices  23 us (24%)
  Pallas kernels  13.9 us (14%)
  waiting for transfers between devices  13.6 us (14%)
    all_to_all x3, blocking collectives, exchange(): return lax.all_to_all(x, axes, split_axis=0, concat_axis=0, tiled=True)  43.4 us
    ppermute x4, starting transfers between devices, exchanged(): return lax.ppermute(x, AXES, pairs).reshape(shape)  23 us
    ppermute x4, waiting for transfers between devices, exchanged(): return lax.ppermute(x, AXES, pairs).reshape(shape)  13.6 us
    pallas_call x1, Pallas kernels, next_basis(): pl.pallas_call(functools.partial(next_kernel, rows_total), out_shape=jax....  7.81 us
    pallas_call x3, Pallas kernels, kernel_call(): pl.pallas_call(body, out_shape=tuple(outs), in_specs=ins, out_specs=(VMEM...  5.69 us
  transfers between devices with their start and end apart: 4, of which 2 were waited for; matrix products, arithmetic and copies ran while one was open for 1% of the time, Pallas kernels for 3%

profile of v5, /device:TPU:1, one launch (start us, length us, event | category | flops | bytes accessed | tf_op | source)
XLA Modules:
  0.0 95.7 jit_solution(1108342159496381367)
XLA Ops:
  0.0 8.7 %collective-permute-start = (bf16[1024,256]{1,0:T(8,128)(2,1)}, bf16[1024,256]{1,0:T(8,128)(2,1)S(1)}, u32[]{:S(2)}, u32[]{:S(2)}) collective-permute-start(bf16[1024,256]{1,0:T(8,128)(2,1)} %param.9), channel_id=1, source_target_pairs={{0,1},{1,0},{2,3},{3,2},{4,5},{5,4},{6,7},{7,6},{8,9},{9,8},{10,11... | collective-permute-start | bytes 1572872 | tf_op jit(solution)/shard_map/ppermute | solution.py:152
  8.7 1.9 %collective-permute-start.1 = (bf16[1024,256]{1,0:T(8,128)(2,1)}, bf16[1024,256]{1,0:T(8,128)(2,1)S(1)}, u32[]{:S(2)}, u32[]{:S(2)}) collective-permute-start(bf16[1024,256]{1,0:T(8,128)(2,1)} %param.9), channel_id=1, source_target_pairs={{0,511},{1,2},{2,1},{3,4},{4,3},{5,6},{6,5},{7,8},{8,7},{9,10},{10... | collective-permute-start | bytes 1572872 | tf_op jit(solution)/shard_map/ppermute | solution.py:152
  11.3 0.7 pad_add_fusion.table
  12.1 0.0 collective-permute-done
  12.1 2.6 %shard_map.55 = (bf16[6,512,512]{2,1,0:T(8,128)(2,1)S(1)}, f32[2,512,256]{2,1,0:T(8,128)S(1)}) custom-call(s32[13]{0:T(128)S(1)} %pad_add_fusion.table, bf16[6,512,512]{2,1,0:T(8,128)(2,1)} %tiles_ref.1, bf16[2,512,256]{2,1,0:T(8,128)(2,1)} %bitcast.15, bf16[2,512,256]{2,1,0:T(8,128)(2,1)S(1)} %bitcast.10), custom_call_target="tpu_custom_call" | custom-call | flops 805306368 | bytes 4194304 | tf_op jit(solution)/shard_map/pallas_call | solution.py:136
  14.7 4.8 %collective-permute-done.1 = bf16[1024,256]{1,0:T(8,128)(2,1)S(1)} collective-permute-done((bf16[1024,256]{1,0:T(8,128)(2,1)}, bf16[1024,256]{1,0:T(8,128)(2,1)S(1)}, u32[]{:S(2)}, u32[]{:S(2)}) %collective-permute-start.1) | collective-permute-done | bytes 524320 | tf_op jit(solution)/shard_map/ppermute | solution.py:152
  19.5 1.6 %shard_map.56 = (bf16[2,512,256]{2,1,0:T(8,128)(2,1)S(1)}, bf16[2,512,256]{2,1,0:T(8,128)(2,1)S(1)}) custom-call(s32[13]{0:T(128)S(1)} %pad_add_fusion.table, bf16[6,512,512]{2,1,0:T(8,128)(2,1)S(1)} %get-tuple-element.15.held_ref, f32[2,512,256]{2,1,0:T(8,128)S(1)} %get-tuple-element.16.acc_in, bf16[2,512,256]{2,1,0:T(8,128)(2,1)S(1)} %bitcast.9), custom_call_target="tpu_custom_call" | custom-call | flops 805306368 | bytes 4194304 | tf_op jit(solution)/shard_map/pallas_call | solution.py:136
  21.1 1.5 %shard_map.57 = (bf16[2,512,256]{2,1,0:T(8,128)(2,1)S(1)}, f32[2,512,256]{2,1,0:T(8,128)S(1)}) custom-call(s32[13]{0:T(128)S(1)} %pad_add_fusion.table, bf16[6,512,512]{2,1,0:T(8,128)(2,1)S(1)} %get-tuple-element.15.held_ref, bf16[2,512,256]{2,1,0:T(8,128)(2,1)S(1)} %get-tuple-element.17.aq_ref), custom_call_target="tpu_custom_call" | custom-call | flops 805306368 | bytes 4194304 | tf_op jit(solution)/shard_map/pallas_call | solution.py:136
  22.6 10.4 %collective-permute-start.3 = (bf16[2,512,256]{2,1,0:T(8,128)(2,1)S(1)}, bf16[2,512,256]{2,1,0:T(8,128)(2,1)S(1)}, u32[]{:S(2)}, u32[]{:S(2)}) collective-permute-start(bf16[2,512,256]{2,1,0:T(8,128)(2,1)S(1)} %get-tuple-element.20), channel_id=1, source_target_pairs={{0,1},{1,0},{2,3},{3,2},{4,5},{5,4},{6,7},{7,6},{8,9},{9,8},{10,11... | collective-permute-start | bytes 1572872 | tf_op jit(solution)/shard_map/ppermute | solution.py:152
  33.0 1.9 %collective-permute-start.2 = (bf16[2,512,256]{2,1,0:T(8,128)(2,1)S(1)}, bf16[2,512,256]{2,1,0:T(8,128)(2,1)S(1)}, u32[]{:S(2)}, u32[]{:S(2)}) collective-permute-start(bf16[2,512,256]{2,1,0:T(8,128)(2,1)S(1)} %get-tuple-element.19), channel_id=1, source_target_pairs={{0,511},{1,2},{2,1},{3,4},{4,3},{5,6},{6,5},{7,8},{8,7},{9,10},{10... | collective-permute-start | bytes 1572872 | tf_op jit(solution)/shard_map/ppermute | solution.py:152
  35.0 0.0 collective-permute-done.3
  35.0 8.9 %collective-permute-done.2 = bf16[2,512,256]{2,1,0:T(8,128)(2,1)S(1)} collective-permute-done((bf16[2,512,256]{2,1,0:T(8,128)(2,1)S(1)}, bf16[2,512,256]{2,1,0:T(8,128)(2,1)S(1)}, u32[]{:S(2)}, u32[]{:S(2)}) %collective-permute-start.2) | collective-permute-done | bytes 524320 | tf_op jit(solution)/shard_map/ppermute | solution.py:152
  43.8 0.4 gram.1
  44.3 13.5 %all_to_all.15 = bf16[16,24,128]{2,1,0:T(8,128)(2,1)S(1)} all-to-all(bf16[16,24,128]{2,1,0:T(8,128)(2,1)S(1)} %bitcast.14), channel_id=1, replica_groups=mesh['z'=8,'y_high'=4,'y_low'=2,'x'=4,'core'=2] {'y_low','x','core'}, dimensions={0} | all-to-all | bytes 196608 | tf_op jit(solution)/shard_map/all_to_all | solution.py:348
  57.8 19.3 %all_to_all.16 = bf16[32,24,128]{2,1,0:T(8,128)(2,1)S(1)} all-to-all(bf16[32,24,128]{2,1,0:T(8,128)(2,1)S(1)} %broadcast_in_dim.6), channel_id=1, replica_groups=mesh['z'=8,'y_high'=4,'y_low'=2,'x'=4,'core'=2] {'z','y_high'}, dimensions={0} | all-to-all | bytes 393216 | tf_op jit(solution)/shard_map/all_to_all | solution.py:348
  77.2 10.6 %all_to_all.17 = bf16[16,24,128]{2,1,0:T(8,128)(2,1)S(1)} all-to-all(bf16[16,24,128]{2,1,0:T(8,128)(2,1)S(1)} %broadcast_in_dim.7), channel_id=1, replica_groups=mesh['z'=8,'y_high'=4,'y_low'=2,'x'=4,'core'=2] {'y_low','x','core'}, dimensions={0} | all-to-all | bytes 196608 | tf_op jit(solution)/shard_map/all_to_all | solution.py:348
  87.8 7.8 %next_basis.1 = f32[1024,256]{1,0:T(8,128)} custom-call(bf16[384,128]{1,0:T(8,128)(2,1)S(1)} %bitcast.13, bf16[1024,128]{1,0:T(8,128)(2,1)S(1)} %get-tuple-element.22.hi_ref, bf16[1024,128]{1,0:T(8,128)(2,1)S(1)} %get-tuple-element.23.lo_ref, f32[1024,128]{1,0:T(8,128)S(1)} %get-tuple-element.24.y_ref), custom_call_target="tpu_custom_call" | custom-call | flops 402653184 | bytes 2097152 | tf_op jit(solution)/shard_map/next_basis/pallas_call | solution.py:324
  (4 shorter events, 0.1 us)
Async XLA Ops:
  0.0 12.1 %collective-permute-start = (bf16[1024,256]{1,0:T(8,128)(2,1)}, bf16[1024,256]{1,0:T(8,128)(2,1)S(1)}, u32[]{:S(2)}, u32[]{:S(2)}) collective-permute-start(bf16[1024,256]{1,0:T(8,128)(2,1)} %param.9), channel_id=1, source_target_pairs={{0,1},{1,0},{2,3},{3,2},{4,5},{5,4},{6,7},{7,6},{8,9},{9,8},{10,11... | collective-permute-start | bytes 1572872 | tf_op jit(solution)/shard_map/ppermute | solution.py:152
  8.7 10.7 %collective-permute-start.1 = (bf16[1024,256]{1,0:T(8,128)(2,1)}, bf16[1024,256]{1,0:T(8,128)(2,1)S(1)}, u32[]{:S(2)}, u32[]{:S(2)}) collective-permute-start(bf16[1024,256]{1,0:T(8,128)(2,1)} %param.9), channel_id=1, source_target_pairs={{0,511},{1,2},{2,1},{3,4},{4,3},{5,6},{6,5},{7,8},{8,7},{9,10},{10... | collective-permute-start | bytes 1572872 | tf_op jit(solution)/shard_map/ppermute | solution.py:152
  22.6 12.4 %collective-permute-start.3 = (bf16[2,512,256]{2,1,0:T(8,128)(2,1)S(1)}, bf16[2,512,256]{2,1,0:T(8,128)(2,1)S(1)}, u32[]{:S(2)}, u32[]{:S(2)}) collective-permute-start(bf16[2,512,256]{2,1,0:T(8,128)(2,1)S(1)} %get-tuple-element.20), channel_id=1, source_target_pairs={{0,1},{1,0},{2,3},{3,2},{4,5},{5,4},{6,7},{7,6},{8,9},{9,8},{10,11... | collective-permute-start | bytes 1572872 | tf_op jit(solution)/shard_map/ppermute | solution.py:152
  33.0 10.8 %collective-permute-start.2 = (bf16[2,512,256]{2,1,0:T(8,128)(2,1)S(1)}, bf16[2,512,256]{2,1,0:T(8,128)(2,1)S(1)}, u32[]{:S(2)}, u32[]{:S(2)}) collective-permute-start(bf16[2,512,256]{2,1,0:T(8,128)(2,1)S(1)} %get-tuple-element.19), channel_id=1, source_target_pairs={{0,511},{1,2},{2,1},{3,4},{4,3},{5,6},{6,5},{7,8},{8,7},{9,10},{10... | collective-permute-start | bytes 1572872 | tf_op jit(solution)/shard_map/ppermute | solution.py:152
